TPU v7x, 16 devices: a 4x2x1 block of a 4x4x8 slice. The times are simulated.
16 devices in a mesh: data: 2 (over y, z), seq: 8 (over x, core).
Axes of the slice: x: 4, y: 2, z: 1, core: 2. Of those that a mesh axis runs over, the one named last changes fastest.
The devices are a block of a 4x4x8 slice.
Arguments:
- tokens: bfloat16 [4, 512, 1024], P('data', 'seq'), parts along dimension 0
- lengths: int32 [4], P('data'), parts along dimension 0
- slot_param: bfloat16 [1024, 1024], replicated
- logit_scale: float32 [], replicated
- w_in: bfloat16 [64, 1024, 4096], P('seq')
- w_out: bfloat16 [64, 4096, 1024], P('seq')
Outputs:
- output: bfloat16 [4, 512, 1024], P('data', 'seq'), parts along dimension 0
There are 2 independent parts. A program takes and returns all parts, laid end to end along the dimension named above; an argument that names none is the same for every part.
All inputs are finite; a program needn't handle non-finite values.
Results may differ from a plain program's by a relative error of at most 0.013898.
Values are sent between devices in bfloat16 or wider.
A program may use at most 768 MiB of HBM per device.

v0:
```python
import jax
import jax.numpy as jnp
from jax import lax
from jax.sharding import PartitionSpec as P

EPSILON = 1e-6
NEG_FILL = -1e30


def l2_normed(values, axis_dim):
    v32 = values.astype(jnp.float32)
    return (v32 * lax.rsqrt(jnp.sum(v32 * v32, axis=axis_dim, keepdims=True) + EPSILON)).astype(jnp.bfloat16)


def solution(mesh):
    seq_size = mesh.shape["seq"]

    def local_layer(tok_blk, len_blk, slot_param, logit_scale, w_in, w_out):
        batch_loc, tok_loc, d_model = tok_blk.shape
        n_slots = slot_param.shape[1]
        exp_loc = w_in.shape[0]
        slot_loc = n_slots // seq_size
        per_exp = slot_loc // exp_loc
        positions = lax.axis_index("seq") * tok_loc + jnp.arange(tok_loc, dtype=jnp.int32)
        tok_valid = (positions[None, :] < len_blk[:, None])[:, :, None]
        logits = logit_scale * jnp.einsum("btd,dn->btn", l2_normed(tok_blk, 2), l2_normed(slot_param, 0), preferred_element_type=jnp.float32)
        masked = jnp.where(tok_valid, logits, NEG_FILL)
        col_max = lax.pmax(jnp.max(masked, axis=1, keepdims=True), "seq")
        disp_w = jnp.exp(masked - col_max)
        col_sum = lax.psum_scatter(jnp.sum(disp_w, axis=1), "seq", scatter_dimension=1, tiled=True)
        part_sum = jnp.einsum("btn,btd->bnd", disp_w.astype(jnp.bfloat16), tok_blk, preferred_element_type=jnp.float32)
        slot_sum = lax.psum_scatter(part_sum.astype(jnp.bfloat16), "seq", scatter_dimension=1, tiled=True)
        slot_in = (slot_sum.astype(jnp.float32) / col_sum[:, :, None]).astype(jnp.bfloat16)
        slot_grp = slot_in.reshape(batch_loc, exp_loc, per_exp, d_model)
        hidden = jax.nn.gelu(jnp.einsum("besd,edf->besf", slot_grp, w_in, preferred_element_type=jnp.float32)).astype(jnp.bfloat16)
        own_out = jnp.einsum("besf,efd->besd", hidden, w_out, preferred_element_type=jnp.float32).astype(jnp.bfloat16)
        slot_out = lax.all_gather(own_out.reshape(batch_loc, slot_loc, d_model), "seq", axis=1, tiled=True)
        comb_w = jnp.exp(logits - jnp.max(logits, axis=2, keepdims=True))
        row_sum = jnp.sum(comb_w, axis=2, keepdims=True)
        tok_mixed = jnp.einsum("btn,bnd->btd", comb_w.astype(jnp.bfloat16), slot_out, preferred_element_type=jnp.float32) / row_sum
        return jnp.where(tok_valid, tok_mixed, 0.0).astype(jnp.bfloat16)

    return jax.shard_map(local_layer, mesh=mesh, in_specs=(P("data", "seq", None), P("data"), P(None, None), P(), P("seq", None, None), P("seq", None, None)), out_specs=P("data", "seq", None), check_vma=False)
```

profile of v0, /device:TPU:113, one launch (start us, length us, event | category | flops | bytes accessed | tf_op | source)
XLA Modules:
  0.0 183.9 jit_solution(11882244975182977539)
XLA Ops:
  6.5 0.0 reduce-scatter.7.cloned.1.call-start
  7.3 1.1 fusion.43
  8.4 2.1 %fusion.8 = f32[1024]{0:T(1024)S(1)} fusion(bf16[1024,1024]{1,0:T(8,128)(2,1)} %param.8), kind=kLoop, calls=%fused_computation.9 | loop fusion | flops 3144704 | bytes 2101248 | tf_op jit(solution)/shard_map/reduce_sum | solution.py:12
  10.4 0.7 broadcast_compare_fusion
  11.2 2.3 %select_reduce_fusion = (f32[2,1024]{1,0:T(2,128)S(1)}, f32[2,64,1024]{2,1,0:T(8,128)S(1)}) fusion(pred[2,64]{1,0:T(4,128)(4,1)S(1)} %broadcast_compare_fusion, bf16[1024,1024]{1,0:T(8,128)(2,1)} %param.8, f32[1024]{0:T(1024)S(1)} %add_rsqrt_fusion, bf16[2,64,1024]{2,1,0:T(8,128)(2,1)} %param.6, f32[2,64]{1,0:T(2,128)S(1)} %add_rsqrt_fusion.1, f32[]{:T(128)S(6)} %copy.18), kind=kOutput, calls=%fused_computation.41 | convolution fusion | flops 272365568 | bytes 2896516 | tf_op jit(solution)/shard_map/btd,dn->btn/dot_general | solution.py:26
  13.5 13.8 %pmax.7 = f32[2,1024]{1,0:T(2,128)S(1)} all-reduce(f32[2,1024]{1,0:T(2,128)S(1)} %get-tuple-element.7), channel_id=1, replica_groups=mesh['data'=2,'seq'=8] {'seq'}, use_global_device_ids=true, to_apply=%region_4.5 | all-reduce | flops 2048 | bytes 16384 | tf_op jit(solution)/shard_map/pmax | solution.py:28
  27.3 0.2 fusion.65
  27.5 1.1 copy.14
  28.5 0.1 reduce-scatter.7.cloned.1.call-update
  28.6 0.1 reduce-scatter.5.cloned.1.call-start
  28.7 3.3 %convolution_convert_fusion = bf16[2,1024,1024]{2,1,0:T(8,128)(2,1)} fusion(bf16[2,64,1024]{2,1,0:T(8,128)(2,1)S(1)} %copy-done, f32[2,64,1024]{2,1,0:T(8,128)S(1)} %get-tuple-element.8, f32[2,1024]{1,0:T(2,128)S(1)} %pmax.7, pred[2,64]{1,0:T(4,128)(4,1)S(1)} %broadcast_compare_fusion), kind=kOutput, calls=%fused_computation.19 | convolution fusion | flops 270925824 | bytes 4989056 | tf_op jit(solution)/shard_map/btn,btd->bnd/dot_general | solution.py:31
  32.0 0.1 reduce-scatter.5.cloned.1.call-update
  32.0 0.1 all-gather.2.cloned.1.call-start
  32.1 22.7 %reduce-scatter.7.cloned.1.call-done = f32[128,2]{1,0:T(8,128)} async-done(((f32[1024,2]{1,0:T(8,128)}), f32[128,2]{1,0:T(8,128)}) %reduce-scatter.7.cloned.1.call-update) | async-done | bytes 1040
  54.9 0.9 copy.15
  55.8 34.1 %reduce-scatter.5.cloned.1.call-done = bf16[2,128,1024]{2,1,0:T(8,128)(2,1)} async-done(((bf16[2,1024,1024]{2,1,0:T(8,128)(2,1)}), bf16[2,128,1024]{2,1,0:T(8,128)(2,1)}) %reduce-scatter.5.cloned.1.call-update) | async-done | bytes 524304 | tf_op jit(solution)/shard_map/reduce_scatter | solution.py:32
  89.8 1.3 divide_convert_fusion
  91.1 25.3 %fusion.5 = f32[2,8,16,4096]{3,2,0,1:T(8,128)} fusion(bf16[8,1024,4096]{2,1,0:T(8,128)(2,1)} %param.10, bf16[2,8,16,1024]{3,2,1,0:T(8,128)(2,1)S(1)} %bitcast.33), kind=kOutput, calls=%fused_computation.6 | convolution fusion | flops 2147483648 | bytes 71827456 | tf_op jit(solution)/shard_map/besd,edf->besf/dot_general | solution.py:35
  116.4 25.7 %fusion.37 = bf16[2,8,16,1024]{3,2,0,1:T(8,128)(2,1)S(1)} fusion(bf16[8,4096,1024]{2,1,0:T(8,128)(2,1)} %param.11, f32[2,8,16,4096]{3,2,0,1:T(8,128)} %fusion.5), kind=kOutput, calls=%fused_computation.31 | convolution fusion | flops 2157182976 | bytes 71827456 | tf_op jit(solution)/shard_map/besf,efd->besd/dot_general | solution.py:36
  142.1 0.8 copy.11
  142.9 0.1 all-gather.2.cloned.1.call-update
  143.0 30.1 %all-gather.2.cloned.1.call-done = bf16[2,1024,1024]{2,1,0:T(8,128)(2,1)} async-done(((bf16[2,128,1024]{2,1,0:T(8,128)(2,1)}), bf16[2,1024,1024]{2,1,0:T(8,128)(2,1)}) %all-gather.2.cloned.1.call-update) | async-done | bytes 4194320 | tf_op jit(solution)/shard_map/all_gather | solution.py:37
  173.0 3.1 %fusion.50 = f32[2,64,1024]{2,1,0:T(8,128)S(1)} fusion(bf16[2,1024,1024]{2,1,0:T(8,128)(2,1)} %all-gather.2.cloned.1.call-done, f32[2,64,1024]{2,1,0:T(8,128)S(1)} %get-tuple-element.8, f32[2,64]{1,0:T(2,128)S(1)} %get-tuple-element.5), kind=kOutput, calls=%fused_computation.46 | convolution fusion | flops 268697600 | bytes 5243392 | tf_op jit(solution)/shard_map/btn,bnd->btd/dot_general | solution.py:40
  176.1 1.3 fusion.42
  (5 shorter events, 0.0 us)
Async XLA Ops:
  6.5 22.1 %copy-start = (bf16[2,64,1024]{2,1,0:T(8,128)(2,1)S(1)}, bf16[2,64,1024]{2,1,0:T(8,128)(2,1)}, u32[]{:S(2)}) copy-start(bf16[2,64,1024]{2,1,0:T(8,128)(2,1)} %param.6) | copy-start | bytes 786436
  6.5 48.3 %reduce-scatter.7.cloned.1.call-start = ((), (), s32[]{:S(2)}) async-start(), calls=%async_computation.4 | async-start | bytes 589824
  28.6 61.2 %reduce-scatter.5.cloned.1.call-start = ((), (), s32[]{:S(2)}) async-start(), calls=%async_computation.2 | async-start | bytes 4718592 | tf_op jit(solution)/shard_map/reduce_scatter | solution.py:32
  32.0 141.0 %all-gather.2.cloned.1.call-start = ((), (), s32[]{:S(2)}) async-start(), calls=%async_computation.3 | async-start | bytes 4718592 | tf_op jit(solution)/shard_map/all_gather | solution.py:37
Sparse Core Ops, SparseCore 0:
  28.7 26.1 reduce-scatter.6
  57.2 32.6 reduce-scatter.4
  143.1 29.8 all-gather.1
where the time goes:
time: 184 us
  waiting for transfers between devices  87 us (47%)
  matrix products  59.7 us (32%)
  between operations  13.9 us (8%)
  blocking collectives  13.8 us (8%)
  other arithmetic  6.64 us (4%)
  local copies, waits for them, and re-layouts  2.79 us (2%)
    reduce_scatter x1, waiting for transfers between devices, local_layer(): lax.psum_scatter(part_sum.astype(jnp.bfloat16), 'seq', scatter_dimension=...  34.1 us
    all_gather x1, waiting for transfers between devices, local_layer(): lax.all_gather(own_out.reshape(batch_loc, slot_loc, d_model), 'seq', axis...  30.1 us
    dot_general x1, matrix products, local_layer(): jnp.einsum('besf,efd->besd', hidden, w_out, preferred_element_type=jnp.fl...  25.7 us
    dot_general x1, matrix products, local_layer(): jnp.einsum('besd,edf->besf', slot_grp, w_in, preferred_element_type=jnp.f...  25.3 us
    unnamed x4, waiting for transfers between devices  22.9 us
    pmax x1, blocking collectives, local_layer(): col_max = lax.pmax(jnp.max(masked, axis=1, keepdims=True), 'seq')  13.8 us
  transfers between devices with their start and end apart: 3, of which 3 were waited for; matrix products, arithmetic and copies ran while one was open for 2% of the time, Pallas kernels for 0%

commit v1 on v0

v1 whole, which is shorter than its diff:
```python
import functools

import jax
import jax.numpy as jnp
from jax import lax
from jax.experimental import pallas as pl
from jax.experimental.pallas import tpu as pltpu
from jax.sharding import PartitionSpec as P

EPSILON = 1e-6
NEG_FILL = -1e30
MESH = pl.DeviceIdType.MESH
F32 = jnp.float32
BF16 = jnp.bfloat16
FF_BLOCK = 1024
AHEAD = 12


def unit_rows(values):
    v32 = values.astype(F32)
    return (v32 * lax.rsqrt(jnp.sum(v32 * v32, axis=1, keepdims=True) + EPSILON)).astype(BF16)


class Exchange:
    def __init__(self, me, n, chunk, send_sem, recv_sem):
        core = lax.rem(me, 2)
        self.me, self.mate = me, me + 1 - 2 * core
        self.right, self.left = lax.rem(me + 2, n), lax.rem(me + n - 2, n)
        self.far = lax.rem(me + n // 2, n)
        self.rightm, self.leftm, self.farm = (p + 1 - 2 * core for p in (self.right, self.left, self.far))
        self.chunk, self.send_sem, self.recv_sem = chunk, send_sem, recv_sem

    def copy(self, i, half, src, to):
        ref = self.chunk(half, src)
        return pltpu.make_async_remote_copy(src_ref=ref, dst_ref=ref, send_sem=self.send_sem(i), recv_sem=self.recv_sem(half, src), device_id={"seq": to}, device_id_type=MESH)

    def plan(self):
        return [(0, self.me, self.right), (1, self.me, self.right), (1, self.me, self.left), (0, self.me, self.left), (0, self.me, self.mate), (1, self.me, self.mate),
                (0, self.left, self.right), (1, self.right, self.left), (0, self.left, self.mate), (1, self.right, self.mate),
                (1, self.left, self.mate), (0, self.right, self.mate), (0, self.far, self.mate), (1, self.far, self.mate)]

    def start(self, first, last):
        for i, (half, src, to) in list(enumerate(self.plan()))[first:last]:
            self.copy(i, half, src, to).start()

    def arrived(self, *pairs):
        for half, src in pairs:
            self.copy(0, half, src, self.mate).wait_recv()

    def own(self):
        self.start(0, 6)

    def first(self):
        self.arrived((0, self.left), (1, self.right))
        self.start(6, 10)

    def second(self):
        self.arrived((1, self.left), (0, self.right))
        self.start(10, 12)

    def third(self):
        self.arrived((0, self.far), (1, self.far))
        self.start(12, 14)

    def from_mate(self, *sources):
        for src in sources:
            self.arrived((0, src), (1, src))

    def sent(self):
        for i, (half, src, to) in enumerate(self.plan()):
            self.copy(i, half, src, to).wait_send()


def kernel(n, tok_hbm, len_ref, phi_hbm, g_ref, w1_hbm, w2_hbm, out_ref, xall, phi, pnt, lt, cbuf, qbuf, cperm, xs, ysall, yexp, yacc, w1buf, w2buf,
           loc_sem, w1_sem, w2_sem, tok_send, tok_recv, ys_send, ys_recv):
    batch, _, toks, d_model = xall.shape
    n_exp, _, rows, _ = ysall.shape
    per_exp = rows // batch
    slot_loc = n_exp * per_exp
    blocks = w1_hbm.shape[2] // FF_BLOCK
    units = n_exp * blocks
    ahead = w1buf.shape[0]
    chips = n // 2
    me = lax.axis_index("seq")
    g = g_ref[0]

    def w_copies(u):
        slot, e = lax.rem(u, ahead), u // blocks
        f0 = pl.multiple_of(lax.rem(u, blocks) * FF_BLOCK, FF_BLOCK)
        return (pltpu.make_async_copy(w1_hbm.at[e, :, pl.ds(f0, FF_BLOCK)], w1buf.at[slot], w1_sem.at[slot]),
                pltpu.make_async_copy(w2_hbm.at[e, pl.ds(f0, FF_BLOCK), :], w2buf.at[slot], w2_sem.at[slot]))

    tok_ex = Exchange(me, n, lambda half, src: xall.at[half, src], lambda i: tok_send.at[i], lambda half, src: tok_recv.at[half, src])
    barrier = pltpu.get_barrier_semaphore()
    for peer in (tok_ex.right, tok_ex.left, tok_ex.mate):
        pl.semaphore_signal(barrier, inc=1, device_id={"seq": peer}, device_id_type=MESH)
    own_in = [pltpu.make_async_copy(tok_hbm.at[b], xall.at[b, me], loc_sem.at[b]) for b in range(batch)]
    for c in own_in:
        c.start()
    phi_in = pltpu.make_async_copy(phi_hbm, phi, loc_sem.at[batch])
    phi_in.start()

    def first_weights(u, _):
        for c in w_copies(u):
            c.start()
        return 0

    lax.fori_loop(0, ahead, first_weights, 0)
    for c in own_in:
        c.wait()
    pl.semaphore_wait(barrier, 3)
    tok_ex.own()

    phi_in.wait()
    d_rows = phi.shape[0]
    n_slots = phi.shape[1]
    step = 64

    def sum_sq(i, acc):
        v = phi[pl.ds(pl.multiple_of(i * step, step), step), :].astype(F32)
        return acc + jnp.sum((v * v).reshape(step // 8, 8, n_slots), axis=0)

    scale = lax.rsqrt(jnp.sum(lax.fori_loop(0, d_rows // step, sum_sq, jnp.zeros((8, n_slots), F32)), axis=0, keepdims=True) + EPSILON)

    def to_unit(i, _):
        at = pl.ds(pl.multiple_of(i * step, step), step)
        phi[at, :] = (phi[at, :].astype(F32) * scale).astype(BF16)
        return 0

    lax.fori_loop(0, d_rows // step, to_unit, 0)
    pnt[...] = phi[:, pl.ds(pl.multiple_of(me * slot_loc, slot_loc), slot_loc)].astype(F32).T.astype(BF16)

    for b in range(batch):
        logits = g * jnp.dot(unit_rows(xall[b, me]), phi[...], preferred_element_type=F32)
        comb = jnp.exp(logits - jnp.max(logits, axis=1, keepdims=True))
        at = pl.ds(b * toks, toks)
        qbuf[at, :] = jnp.broadcast_to(jnp.sum(comb, axis=1, keepdims=True), (toks, 128))
        cbuf[at, :] = comb.astype(BF16)

    tok_ex.first()

    def per_expert(e, _):
        j = lax.broadcasted_iota(jnp.int32, (n_slots, slot_loc), 0)
        k = lax.broadcasted_iota(jnp.int32, (n_slots, slot_loc), 1)
        pick = (j == (k // per_exp) * slot_loc + e * per_exp + lax.rem(k, per_exp)).astype(F32).astype(BF16)
        cperm[e] = jnp.dot(cbuf[...], pick, preferred_element_type=F32).astype(BF16)
        return 0

    lax.fori_loop(0, n_exp, per_expert, 0)

    def chip_logits(chip):
        for b in range(batch):
            x_chip = xall[b, pl.ds(2 * chip, 2)].reshape(2 * toks, d_model)
            logits = g * lax.dot_general(pnt[...], unit_rows(x_chip), (((1,), (1,)), ((), ())), preferred_element_type=F32)
            pos = chip * (2 * toks) + lax.broadcasted_iota(jnp.int32, logits.shape, 1)
            lt[b, chip] = jnp.where(pos < len_ref[b], logits, NEG_FILL)

    tok_ex.from_mate(tok_ex.mate)
    chip_logits(me // 2)
    tok_ex.second()
    tok_ex.from_mate(tok_ex.leftm, tok_ex.rightm)
    chip_logits(tok_ex.left // 2)
    chip_logits(tok_ex.right // 2)
    tok_ex.third()
    tok_ex.from_mate(tok_ex.farm)
    chip_logits(tok_ex.far // 2)

    for b in range(batch):
        parts = [lt[b, k] for k in range(chips)]
        top = jnp.max(functools.reduce(jnp.maximum, parts), axis=1, keepdims=True)
        disp = [jnp.exp(p - top) for p in parts]
        col_sum = jnp.sum(functools.reduce(jnp.add, disp), axis=1, keepdims=True)
        weights = jnp.concatenate([w.astype(BF16) for w in disp], axis=1)
        slot_sum = jnp.dot(weights, xall[b].reshape(n * toks, d_model), preferred_element_type=F32)
        xs[:, pl.ds(b * per_exp, per_exp), :] = (slot_sum / col_sum).astype(BF16).reshape(n_exp, per_exp, d_model)
    tok_ex.sent()
    yacc[...] = jnp.zeros_like(yacc)

    def ys_ex(e):
        return Exchange(me, n, lambda half, src: ysall.at[e, src, pl.ds(half * per_exp, per_exp)], lambda i: ys_send.at[lax.rem(e, 2), i], lambda half, src: ys_recv.at[e, half, src])

    def combine(e):
        for b in range(batch):
            at = pl.ds(b * toks, toks)
            got = ysall[e, :, pl.ds(b * per_exp, per_exp), :].reshape(n * per_exp, d_model)
            yacc[at, :] += jnp.dot(cperm[e, at, :], got, preferred_element_type=F32)

    def finish(e):
        ex = ys_ex(e)
        ex.from_mate(ex.mate, ex.leftm, ex.rightm, ex.farm)
        combine(e)
        ex.sent()

    def expert(e, _):
        for j in range(blocks):
            u = e * blocks + j
            slot = lax.rem(u, ahead)
            c1, c2 = w_copies(u)
            c1.wait()
            hidden = jax.nn.gelu(jnp.dot(xs[e], w1buf[slot], preferred_element_type=F32)).astype(BF16)
            c2.wait()
            part = jnp.dot(hidden, w2buf[slot], preferred_element_type=F32)
            if j == 0:
                yexp[...] = part
            else:
                yexp[...] += part

            @pl.when(u + ahead < units)
            def _():
                for c in w_copies(u + ahead):
                    c.start()

            if j == 0:
                @pl.when(e >= 1)
                def _():
                    ys_ex(e - 1).own()
            if j == 1:
                @pl.when(e >= 2)
                def _():
                    ys_ex(e - 2).third()
            if j == 2:
                @pl.when(e >= 2)
                def _():
                    finish(e - 2)
            if j == 3:
                @pl.when(e >= 1)
                def _():
                    ys_ex(e - 1).first()
                    ys_ex(e - 1).second()
        ysall[e, me] = yexp[...].astype(BF16)
        return 0

    lax.fori_loop(0, n_exp, expert, 0)
    ys_ex(n_exp - 1).own()
    ys_ex(n_exp - 2).third()
    finish(n_exp - 2)
    ys_ex(n_exp - 1).first()
    ys_ex(n_exp - 1).second()
    ys_ex(n_exp - 1).third()
    finish(n_exp - 1)

    for b in range(batch):
        at = pl.ds(b * toks, toks)
        pos = me * toks + lax.broadcasted_iota(jnp.int32, (toks, 1), 0)
        out_ref[b] = jnp.where(pos < len_ref[b], yacc[at, :] / qbuf[at, 0:1], 0.0).astype(BF16)


def solution(mesh):
    n = mesh.shape["seq"]

    def local_layer(tok_blk, len_blk, slot_param, logit_scale, w_in, w_out):
        batch, toks, d_model = tok_blk.shape
        n_slots = slot_param.shape[1]
        n_exp = w_in.shape[0]
        slot_loc = n_slots // n
        rows = batch * (slot_loc // n_exp)
        dma = pltpu.SemaphoreType.DMA
        any_spec = pl.BlockSpec(memory_space=pl.ANY)
        smem_spec = pl.BlockSpec(memory_space=pltpu.SMEM)
        return pl.pallas_call(
            functools.partial(kernel, n),
            out_shape=jax.ShapeDtypeStruct(tok_blk.shape, BF16),
            in_specs=[any_spec, smem_spec, any_spec, smem_spec, any_spec, any_spec],
            out_specs=pl.BlockSpec(memory_space=pltpu.VMEM),
            scratch_shapes=[
                pltpu.VMEM((batch, n, toks, d_model), BF16),
                pltpu.VMEM(slot_param.shape, BF16),
                pltpu.VMEM((slot_loc, d_model), BF16),
                pltpu.VMEM((batch, n // 2, slot_loc, 2 * toks), F32),
                pltpu.VMEM((batch * toks, n_slots), BF16),
                pltpu.VMEM((batch * toks, 128), F32),
                pltpu.VMEM((n_exp, batch * toks, n_slots // n_exp), BF16),
                pltpu.VMEM((n_exp, rows, d_model), BF16),
                pltpu.VMEM((n_exp, n, rows, d_model), BF16),
                pltpu.VMEM((rows, d_model), F32),
                pltpu.VMEM((batch * toks, d_model), F32),
                pltpu.VMEM((AHEAD, d_model, FF_BLOCK), BF16),
                pltpu.VMEM((AHEAD, FF_BLOCK, d_model), BF16),
                dma((batch + 1,)), dma((AHEAD,)), dma((AHEAD,)),
                dma((14,)), dma((batch, n)), dma((2, 14)), dma((n_exp, batch, n)),
            ],
            compiler_params=pltpu.CompilerParams(collective_id=0, has_side_effects=True, vmem_limit_bytes=67043328),
        )(tok_blk, len_blk, slot_param, logit_scale.reshape(1), w_in, w_out)

    return jax.shard_map(local_layer, mesh=mesh, in_specs=(P("data", "seq", None), P("data"), P(None, None), P(), P("seq", None, None), P("seq", None, None)), out_specs=P("data", "seq", None), check_vma=False)
```

time: 184 us -> 75.5 us (0.41)
  waiting for transfers between devices: 87 us -> 0 us
  Pallas kernels: 0 us -> 73 us
  matrix products: 59.7 us -> 0 us
  blocking collectives: 13.8 us -> 0 us
  between operations: 13.9 us -> 0.66 us
  other arithmetic: 6.64 us -> 0 us
    pallas_call x0 -> x1, Pallas kernels: none -> 73 us  [local_layer(): pl.pallas_call(functools.partial(kernel, n), out_shape=jax.ShapeDtypeStru...]
    dot_general x5 -> x0, matrix products: 59.7 us -> none  [the longest x1 25.7 us: local_layer(): jnp.einsum('besf,efd->besd', hidden, w_out, preferred_element_type=jnp.fl...]
    reduce_scatter x1 -> x0, waiting for transfers between devices: 34.1 us -> none  [local_layer(): lax.psum_scatter(part_sum.astype(jnp.bfloat16), 'seq', scatter_dimension=...]
    all_gather x1 -> x0, waiting for transfers between devices: 30.1 us -> none  [local_layer(): lax.all_gather(own_out.reshape(batch_loc, slot_loc, d_model), 'seq', axis...]
    unnamed x4 -> x0, waiting for transfers between devices: 22.9 us -> none
    pmax x1 -> x0, blocking collectives: 13.8 us -> none  [local_layer(): col_max = lax.pmax(jnp.max(masked, axis=1, keepdims=True), 'seq')]
    reduce_sum x2 -> x0, other arithmetic: 3.16 us -> none  [l2_normed(): jnp.sum(v32 * v32, axis=axis_dim, keepdims=True) + EPSILON]
  transfers between devices with their start and end apart: 3 -> 0, of which waited for: 3 -> 0; matrix products, arithmetic and copies ran while one was open for 2% -> 0% of each run, Pallas kernels for 0% -> 0%
where the time goes in v1:
time: 75.5 us; the launch traced here: 75.4 us
  Pallas kernels  73 us (97%)
  local copies, waits for them, and re-layouts  1.67 us (2%)
    pallas_call x1, Pallas kernels, local_layer(): pl.pallas_call(functools.partial(kernel, n), out_shape=jax.ShapeDtypeStru...  73 us
    unnamed x1, local copies, waits for them, and re-layouts  1.67 us

profile of v1, /device:TPU:113, one launch (start us, length us, event | category | flops | bytes accessed | tf_op | source)
XLA Modules:
  0.0 75.4 jit_solution(1151039396961452547)
XLA Ops:
  0.7 73.0 %shard_map.64 = bf16[2,64,1024]{2,1,0:T(8,128)(2,1)} custom-call(bf16[2,64,1024]{2,1,0:T(8,128)(2,1)} %tok_hbm.1, s32[2]{0:T(128)} %len_ref.1, bf16[1024,1024]{1,0:T(8,128)(2,1)} %phi_hbm.1, f32[1]{0:T(128)} %bitcast.1.g_ref, bf16[8,1024,4096]{2,1,0:T(8,128)(2,1)} %w1_hbm.1, bf16[8,4096,1024]{2,1,0:T(8,128)(2,1)} %w2_hbm.1), custom_call_target="tpu_custom_call" | custom-call | tf_op jit(solution)/shard_map/pallas_call | solution.py:260
  73.7 1.7 %copy.9 = bf16[2,64,1024]{2,1,0:T(8,128)(2,1)} copy(bf16[2,64,1024]{2,1,0:T(8,128)(2,1)} %shard_map.64) | data formatting | bytes 524288

commit v2 on v1

--- a/solution.py
+++ b/solution.py
@@ -13,7 +13,11 @@
 F32 = jnp.float32
 BF16 = jnp.bfloat16
 FF_BLOCK = 1024
+JOBS = "UAAAU"
+ORDER = (("U", 0), ("A", 0), ("A", 1), ("P", 0), ("A", 2), ("P", 1), ("U", 1), ("P", 2))
+SCHEDULE = {4: "o0", 8: "o1", 9: "f0", 12: "o2", 13: "f1 o3", 14: "t0", 16: "m0 o4", 17: "t1 f2 o5", 18: "f3", 19: "m1", 20: "o6 t2 f4 t3 o7 f5 m2 f6 m3 t4 f7 t5 m4 t6 m5 t7 m6 m7"}
 AHEAD = 12
+VMEM_BYTES = 62 * 1024 * 1024
 
 
 def unit_rows(values):
@@ -71,45 +75,63 @@
             self.copy(i, half, src, to).wait_send()
 
 
-def kernel(n, tok_hbm, len_ref, phi_hbm, g_ref, w1_hbm, w2_hbm, out_ref, xall, phi, pnt, lt, cbuf, qbuf, cperm, xs, ysall, yexp, yacc, w1buf, w2buf,
-           loc_sem, w1_sem, w2_sem, tok_send, tok_recv, ys_send, ys_recv):
+def kernel(n, tok_hbm, len_ref, phi_hbm, g_ref, w1_hbm, w2_hbm, out_ref, xall, phi, pnt, lt, cbuf, qbuf, cperm, xs, xpair, ysall, yback, hidden, yexp, yacc, w1buf, w2buf,
+           loc_sem, w1_sem, w2_sem, tok_send, tok_recv, ys_send, ys_recv, xp_send, xp_recv, yb_send, yb_recv):
     batch, _, toks, d_model = xall.shape
     n_exp, _, rows, _ = ysall.shape
     per_exp = rows // batch
     slot_loc = n_exp * per_exp
     blocks = w1_hbm.shape[2] // FF_BLOCK
-    units = n_exp * blocks
     ahead = w1buf.shape[0]
     chips = n // 2
     me = lax.axis_index("seq")
     g = g_ref[0]
 
-    def w_copies(u):
-        slot, e = lax.rem(u, ahead), u // blocks
-        f0 = pl.multiple_of(lax.rem(u, blocks) * FF_BLOCK, FF_BLOCK)
-        return (pltpu.make_async_copy(w1_hbm.at[e, :, pl.ds(f0, FF_BLOCK)], w1buf.at[slot], w1_sem.at[slot]),
-                pltpu.make_async_copy(w2_hbm.at[e, pl.ds(f0, FF_BLOCK), :], w2buf.at[slot], w2_sem.at[slot]))
+    data = lax.axis_index("data")
+    odd = lax.rem(data, 2)
+    pair = data + 1 - 2 * odd
+    shared = JOBS.count("A")
+
+    def expert_of(kind, k):
+        if kind == "U":
+            return k if k < JOBS.index("A") else k + 2 * shared
+        return JOBS.index("A") + shared * (odd if kind == "A" else 1 - odd) + k
+
+    job_of = [(kind, JOBS[:i].count(kind)) for i, kind in enumerate(JOBS)]
+    units = len(JOBS) * blocks
+
+    def w1_copy(u):
+        e, f0 = expert_of(*job_of[u // blocks]), u % blocks * FF_BLOCK
+        return pltpu.make_async_copy(w1_hbm.at[e, :, pl.ds(f0, FF_BLOCK)], w1buf.at[u % ahead], w1_sem.at[u % ahead])
+
+    def w2_copy(u):
+        e, f0 = expert_of(*job_of[u // blocks]), u % blocks * FF_BLOCK
+        return pltpu.make_async_copy(w2_hbm.at[e, pl.ds(f0, FF_BLOCK), :], w2buf.at[u % ahead], w2_sem.at[u % ahead])
+
+    def x_to_pair(k):
+        return pltpu.make_async_remote_copy(src_ref=xs.at[expert_of("P", k)], dst_ref=xpair.at[k, pl.ds(rows, rows)], send_sem=xp_send.at[k], recv_sem=xp_recv.at[k], device_id={"data": pair}, device_id_type=MESH)
+
+    def y_to_pair(k):
+        return pltpu.make_async_remote_copy(src_ref=yback.at[k], dst_ref=ysall.at[ORDER.index(("P", k)), me], send_sem=yb_send.at[k], recv_sem=yb_recv.at[k], device_id={"data": pair}, device_id_type=MESH)
 
     tok_ex = Exchange(me, n, lambda half, src: xall.at[half, src], lambda i: tok_send.at[i], lambda half, src: tok_recv.at[half, src])
     barrier = pltpu.get_barrier_semaphore()
     for peer in (tok_ex.right, tok_ex.left, tok_ex.mate):
         pl.semaphore_signal(barrier, inc=1, device_id={"seq": peer}, device_id_type=MESH)
+    pl.semaphore_signal(barrier, inc=1, device_id={"data": pair}, device_id_type=MESH)
     own_in = [pltpu.make_async_copy(tok_hbm.at[b], xall.at[b, me], loc_sem.at[b]) for b in range(batch)]
     for c in own_in:
         c.start()
     phi_in = pltpu.make_async_copy(phi_hbm, phi, loc_sem.at[batch])
     phi_in.start()
 
-    def first_weights(u, _):
-        for c in w_copies(u):
-            c.start()
-        return 0
-
-    lax.fori_loop(0, ahead, first_weights, 0)
     for c in own_in:
         c.wait()
-    pl.semaphore_wait(barrier, 3)
+    pl.semaphore_wait(barrier, 4)
     tok_ex.own()
+    for u in range(min(ahead, units)):
+        w1_copy(u).start()
+        w2_copy(u).start()
 
     phi_in.wait()
     d_rows = phi.shape[0]
@@ -139,14 +161,15 @@
 
     tok_ex.first()
 
-    def per_expert(e, _):
+    def regroup():
         j = lax.broadcasted_iota(jnp.int32, (n_slots, slot_loc), 0)
         k = lax.broadcasted_iota(jnp.int32, (n_slots, slot_loc), 1)
-        pick = (j == (k // per_exp) * slot_loc + e * per_exp + lax.rem(k, per_exp)).astype(F32).astype(BF16)
-        cperm[e] = jnp.dot(cbuf[...], pick, preferred_element_type=F32).astype(BF16)
-        return 0
-
-    lax.fori_loop(0, n_exp, per_expert, 0)
+        first = j - ((k // per_exp) * slot_loc + lax.rem(k, per_exp))
+        for r, what in enumerate(ORDER):
+            pick = (first == expert_of(*what) * per_exp).astype(F32).astype(BF16)
+            cperm[r] = jnp.dot(cbuf[...], pick, preferred_element_type=F32).astype(BF16)
+
+    regroup()
 
     def chip_logits(chip):
         for b in range(batch):
@@ -173,71 +196,77 @@
         weights = jnp.concatenate([w.astype(BF16) for w in disp], axis=1)
         slot_sum = jnp.dot(weights, xall[b].reshape(n * toks, d_model), preferred_element_type=F32)
         xs[:, pl.ds(b * per_exp, per_exp), :] = (slot_sum / col_sum).astype(BF16).reshape(n_exp, per_exp, d_model)
+    for k in range(shared):
+        x_to_pair(k).start()
+        xpair[k, pl.ds(0, rows)] = xs[expert_of("A", k)]
     tok_ex.sent()
     yacc[...] = jnp.zeros_like(yacc)
 
-    def ys_ex(e):
-        return Exchange(me, n, lambda half, src: ysall.at[e, src, pl.ds(half * per_exp, per_exp)], lambda i: ys_send.at[lax.rem(e, 2), i], lambda half, src: ys_recv.at[e, half, src])
-
-    def combine(e):
+    def ys_ex(r):
+        return Exchange(me, n, lambda half, src: ysall.at[r, src, pl.ds(half * per_exp, per_exp)], lambda i: ys_send.at[r, i], lambda half, src: ys_recv.at[r, half, src])
+
+    def combine(r):
         for b in range(batch):
             at = pl.ds(b * toks, toks)
-            got = ysall[e, :, pl.ds(b * per_exp, per_exp), :].reshape(n * per_exp, d_model)
-            yacc[at, :] += jnp.dot(cperm[e, at, :], got, preferred_element_type=F32)
-
-    def finish(e):
-        ex = ys_ex(e)
-        ex.from_mate(ex.mate, ex.leftm, ex.rightm, ex.farm)
-        combine(e)
-        ex.sent()
-
-    def expert(e, _):
-        for j in range(blocks):
-            u = e * blocks + j
-            slot = lax.rem(u, ahead)
-            c1, c2 = w_copies(u)
-            c1.wait()
-            hidden = jax.nn.gelu(jnp.dot(xs[e], w1buf[slot], preferred_element_type=F32)).astype(BF16)
-            c2.wait()
-            part = jnp.dot(hidden, w2buf[slot], preferred_element_type=F32)
-            if j == 0:
-                yexp[...] = part
-            else:
-                yexp[...] += part
-
-            @pl.when(u + ahead < units)
-            def _():
-                for c in w_copies(u + ahead):
-                    c.start()
-
-            if j == 0:
-                @pl.when(e >= 1)
-                def _():
-                    ys_ex(e - 1).own()
-            if j == 1:
-                @pl.when(e >= 2)
-                def _():
-                    ys_ex(e - 2).third()
-            if j == 2:
-                @pl.when(e >= 2)
-                def _():
-                    finish(e - 2)
-            if j == 3:
-                @pl.when(e >= 1)
-                def _():
-                    ys_ex(e - 1).first()
-                    ys_ex(e - 1).second()
-        ysall[e, me] = yexp[...].astype(BF16)
-        return 0
-
-    lax.fori_loop(0, n_exp, expert, 0)
-    ys_ex(n_exp - 1).own()
-    ys_ex(n_exp - 2).third()
-    finish(n_exp - 2)
-    ys_ex(n_exp - 1).first()
-    ys_ex(n_exp - 1).second()
-    ys_ex(n_exp - 1).third()
-    finish(n_exp - 1)
+            got = ysall[r, :, pl.ds(b * per_exp, per_exp), :].reshape(n * per_exp, d_model)
+            yacc[at, :] += jnp.dot(cperm[r, at, :], got, preferred_element_type=F32)
+
+    def act(what):
+        kind, r = what[0], int(what[1:])
+        ex = ys_ex(r)
+        with jax.named_scope(what):
+            if kind == "o":
+                if ORDER[r][0] == "P":
+                    y_to_pair(ORDER[r][1]).wait_recv()
+                ex.own()
+            if kind == "f":
+                ex.first()
+                ex.second()
+            if kind == "t":
+                ex.third()
+            if kind == "m":
+                ex.from_mate(ex.mate, ex.leftm, ex.rightm, ex.farm)
+                combine(r)
+
+    for b in range(units + 1):
+        with jax.named_scope(f"block{b}"):
+            if b < units:
+                kind, k = job_of[b // blocks]
+                if kind == "A" and b % blocks == 0:
+                    x_to_pair(k).wait_recv()
+                w1_copy(b).wait()
+            if b > 0:
+                w2_copy(b - 1).wait()
+            if b < units:
+                x_job = xs[expert_of(kind, k)] if kind == "U" else xpair[k]
+                pre = jnp.dot(x_job, w1buf[b % ahead], preferred_element_type=F32)
+            if b > 0:
+                done, dk = job_of[(b - 1) // blocks]
+                live = pl.ds(0, rows if done == "U" else 2 * rows)
+                part = jnp.dot(hidden[(b - 1) % 2, live, :], w2buf[(b - 1) % ahead], preferred_element_type=F32)
+                if (b - 1) % blocks:
+                    part = yexp[live, :] + part
+                if b % blocks:
+                    yexp[live, :] = part
+                else:
+                    ysall[ORDER.index((done, dk)), me] = part[:rows].astype(BF16)
+                    if done == "A":
+                        yback[dk] = part[rows:].astype(BF16)
+            if b < units:
+                hidden[b % 2, pl.ds(0, pre.shape[0]), :] = jax.nn.gelu(pre).astype(BF16)
+        if b + ahead < units:
+            w1_copy(b + ahead).start()
+        if 0 < b <= units - ahead:
+            w2_copy(b - 1 + ahead).start()
+        if b > 0 and b % blocks == 0 and done == "A":
+            y_to_pair(dk).start()
+        for what in SCHEDULE.get(b, "").split():
+            act(what)
+    for r in range(n_exp):
+        ys_ex(r).sent()
+    for k in range(shared):
+        x_to_pair(k).wait_send()
+        y_to_pair(k).wait_send()
 
     for b in range(batch):
         at = pl.ds(b * toks, toks)
@@ -259,7 +288,7 @@
         smem_spec = pl.BlockSpec(memory_space=pltpu.SMEM)
         return pl.pallas_call(
             functools.partial(kernel, n),
-            out_shape=jax.ShapeDtypeStruct(tok_blk.shape, BF16),
+            out_shape=pltpu.VMEM(tok_blk.shape, BF16),
             in_specs=[any_spec, smem_spec, any_spec, smem_spec, any_spec, any_spec],
             out_specs=pl.BlockSpec(memory_space=pltpu.VMEM),
             scratch_shapes=[
@@ -271,15 +300,19 @@
                 pltpu.VMEM((batch * toks, 128), F32),
                 pltpu.VMEM((n_exp, batch * toks, n_slots // n_exp), BF16),
                 pltpu.VMEM((n_exp, rows, d_model), BF16),
+                pltpu.VMEM((JOBS.count("A"), 2 * rows, d_model), BF16),
                 pltpu.VMEM((n_exp, n, rows, d_model), BF16),
-                pltpu.VMEM((rows, d_model), F32),
+                pltpu.VMEM((JOBS.count("A"), rows, d_model), BF16),
+                pltpu.VMEM((2, 2 * rows, FF_BLOCK), BF16),
+                pltpu.VMEM((2 * rows, d_model), F32),
                 pltpu.VMEM((batch * toks, d_model), F32),
                 pltpu.VMEM((AHEAD, d_model, FF_BLOCK), BF16),
                 pltpu.VMEM((AHEAD, FF_BLOCK, d_model), BF16),
                 dma((batch + 1,)), dma((AHEAD,)), dma((AHEAD,)),
-                dma((14,)), dma((batch, n)), dma((2, 14)), dma((n_exp, batch, n)),
+                dma((14,)), dma((batch, n)), dma((n_exp, 14)), dma((n_exp, batch, n)),
+                *[dma((JOBS.count("A"),))] * 4,
             ],
-            compiler_params=pltpu.CompilerParams(collective_id=0, has_side_effects=True, vmem_limit_bytes=67043328),
+            compiler_params=pltpu.CompilerParams(collective_id=0, has_side_effects=True, vmem_limit_bytes=VMEM_BYTES),
         )(tok_blk, len_blk, slot_param, logit_scale.reshape(1), w_in, w_out)
 
     return jax.shard_map(local_layer, mesh=mesh, in_specs=(P("data", "seq", None), P("data"), P(None, None), P(), P("seq", None, None), P("seq", None, None)), out_specs=P("data", "seq", None), check_vma=False)

time: 75.5 us -> 53.9 us (0.71)
  Pallas kernels: 73 us -> 52.4 us
  local copies, waits for them, and re-layouts: 1.67 us -> 0.71 us
    pallas_call x1, Pallas kernels: 73 us -> 52.4 us  [local_layer(): pl.pallas_call(functools.partial(kernel, n), out_shape=pltpu.VMEM(tok_blk...]
    unnamed x1, local copies, waits for them, and re-layouts: 1.67 us -> 0.71 us
where the time goes in v2:
time: 53.9 us; the launch traced here: 53.7 us
  Pallas kernels  52.4 us (97%)
  local copies, waits for them, and re-layouts  0.71 us (1%)
  between operations  0.66 us (1%)
    pallas_call x1, Pallas kernels, local_layer(): pl.pallas_call(functools.partial(kernel, n), out_shape=pltpu.VMEM(tok_blk...  52.4 us

profile of v2, /device:TPU:113, one launch (start us, length us, event | category | flops | bytes accessed | tf_op | source)
XLA Modules:
  0.0 53.7 jit_solution(15392555812841692897)
XLA Ops:
  0.7 52.4 %shard_map.64 = bf16[2,64,1024]{2,1,0:T(8,128)(2,1)S(1)} custom-call(bf16[2,64,1024]{2,1,0:T(8,128)(2,1)} %tok_hbm.1, s32[2]{0:T(128)} %len_ref.1, bf16[1024,1024]{1,0:T(8,128)(2,1)} %phi_hbm.1, f32[1]{0:T(128)} %bitcast.1.g_ref, bf16[8,1024,4096]{2,1,0:T(8,128)(2,1)} %w1_hbm.1, bf16[8,4096,1024]{2,1,0:T(8,128)(2,1)} %w2_hbm.1), custom_call_target="tpu_custom_call" | custom-call | tf_op jit(solution)/shard_map/pallas_call | solution.py:289
  53.0 0.7 %copy.8 = bf16[2,64,1024]{2,1,0:T(8,128)(2,1)} copy(bf16[2,64,1024]{2,1,0:T(8,128)(2,1)S(1)} %shard_map.64) | data formatting | bytes 524288

commit v3 on v2

v3 whole, which is shorter than its diff:
```python
import functools

import jax
import jax.numpy as jnp
from jax import lax
from jax.experimental import pallas as pl
from jax.experimental.pallas import tpu as pltpu
from jax.sharding import PartitionSpec as P

EPSILON = 1e-6
NEG_FILL = -1e30
MESH = pl.DeviceIdType.MESH
F32 = jnp.float32
BF16 = jnp.bfloat16
FF_BLOCK = 1024
JOBS = (("U", 0, 0), ("U", 1, None), ("A", 0, None), ("A", 1, None), ("A", 2, None), ("U", 0, 1))
EXPERTS = (("U", 0), ("A", 0), ("A", 1), ("P", 0), ("A", 2), ("P", 1), ("U", 1), ("P", 2))
RINGS = (("U", 0, 0), ("U", 1, None), ("A", 0, None), ("A", 1, None), ("P", 0, None), ("A", 2, None), ("P", 1, None), ("U", 0, 1), ("P", 2, None))
BEFORE, SHARED = 1, 3
PROGRAM = (
    "B2", "S1", "B1", "T1", "B1", "L1", "D1", "B1", "o0", "B1", "B1", "B1", "B1", "f0", "s0", "o1", "B1", "B1", "B1", "B1", "t0", "o2",
    "B1", "f1", "B1", "m0", "s1", "B1", "B1", "o3", "f2", "B1", "o4", "s2", "B1", "t1", "B1", "B1", "o5", "m1", "f3", "B1", "o6", "s3",
    "B2", "t2", "B1", "f4", "o7", "s4", "t3", "o8", "f5", "s5", "m2", "f6", "s6", "t4", "f7", "s7", "m3", "f8", "s8", "t5", "t6", "m4",
    "t7", "t8", "m5", "m6", "m7", "m8",
)
AHEAD = 12
VMEM_BYTES = 62 * 1024 * 1024


def unit_rows(values):
    v32 = values.astype(F32)
    return (v32 * lax.rsqrt(jnp.sum(v32 * v32, axis=1, keepdims=True) + EPSILON)).astype(BF16)


FIRST, SECOND, THIRD, MATE, MATE_NEAR, MATE_FAR = range(6)


class Exchange:
    def __init__(self, me, n, chunk, span, send_sem, recv_sem, groups):
        core = lax.rem(me, 2)
        self.me, self.mate = me, me + 1 - 2 * core
        self.right, self.left = lax.rem(me + 2, n), lax.rem(me + n - 2, n)
        self.far = lax.rem(me + n // 2, n)
        self.chunk, self.span, self.send_sem, self.recv_sem, self.groups = chunk, span, send_sem, recv_sem, groups

    def plan(self):
        me, right, left, far, mate = self.me, self.right, self.left, self.far, self.mate
        return [(0, me, right, FIRST), (1, me, right, SECOND), (1, me, left, FIRST), (0, me, left, SECOND), (0, me, mate, MATE), (1, me, mate, MATE),
                (0, left, right, THIRD), (1, right, left, THIRD), (0, left, mate, MATE_NEAR), (1, right, mate, MATE_NEAR),
                (1, left, mate, MATE_NEAR), (0, right, mate, MATE_NEAR), (0, far, mate, MATE_FAR), (1, far, mate, MATE_FAR)]

    def start(self, *which):
        for half, src, to, group in (self.plan()[i] for i in which):
            ref = self.chunk(half, src)
            pltpu.make_async_remote_copy(src_ref=ref, dst_ref=ref, send_sem=self.send_sem, recv_sem=self.recv_sem(self.groups[group]), device_id={"seq": to}, device_id_type=MESH).start()

    def arrived(self, group, pairs):
        ref = self.span(pairs)
        pltpu.make_async_remote_copy(src_ref=ref, dst_ref=ref, send_sem=self.send_sem, recv_sem=self.recv_sem(group), device_id={"seq": self.mate}, device_id_type=MESH).wait_recv()

    def own(self):
        self.start(0, 1, 2, 3, 4, 5)

    def first(self):
        self.arrived(FIRST, 1)
        self.start(6, 7, 8, 9)

    def second(self):
        self.arrived(SECOND, 1)
        self.start(10, 11)

    def third(self):
        self.arrived(THIRD, 1)
        self.start(12, 13)

    def sent(self):
        ref = self.span(7)
        pltpu.make_async_remote_copy(src_ref=ref, dst_ref=ref, send_sem=self.send_sem, recv_sem=self.recv_sem(0), device_id={"seq": self.mate}, device_id_type=MESH).wait_send()


def kernel(n, tok_hbm, len_hbm, phi_hbm, g_ref, w1_hbm, w2_hbm, out_ref, xall, phi, pnt, lt, cbuf, qbuf, cperm, xs, xpair, ysall, yback, hidden, yexp, yacc, w1buf, w2buf,
           loc_sem, w1_sem, w2_sem, tok_send, tok_recv, ys_send, ys_recv, xp_send, xp_recv, yb_send, yb_recv, len_ref):
    batch, _, toks, d_model = xall.shape
    n_exp, _, rows, _ = ysall.shape
    per_exp = rows // batch
    slot_loc = n_exp * per_exp
    blocks = w1_hbm.shape[2] // FF_BLOCK
    ahead = w1buf.shape[0]
    chips = n // 2
    me = lax.axis_index("seq")
    g = g_ref[0]

    data = lax.axis_index("data")
    odd = lax.rem(data, 2)
    pair = data + 1 - 2 * odd

    def expert_of(kind, k):
        if kind == "U":
            return k if k < BEFORE else k + 2 * SHARED
        return BEFORE + SHARED * (odd if kind == "A" else 1 - odd) + k

    loads = list(dict.fromkeys((kind, k) for kind, k, _ in JOBS))
    n_loads = len(loads) * blocks
    units = len(JOBS) * blocks

    def job_of(b):
        return JOBS[b // blocks]

    def load_of(b):
        return loads.index(job_of(b)[:2]) * blocks + b % blocks

    def used_again(b):
        return any(load_of(later) == load_of(b) for later in range(b + 1, units))

    def used_before(b):
        return any(load_of(early) == load_of(b) for early in range(b))

    def slot_of(u):
        return u if u < ahead else blocks + (u - ahead) % (ahead - blocks)

    def next_load(u):
        return next((v for v in range(u + 1, n_loads) if slot_of(v) == slot_of(u)), None)

    def w1_copy(u):
        e, f0 = expert_of(*loads[u // blocks]), u % blocks * FF_BLOCK
        return pltpu.make_async_copy(w1_hbm.at[e, :, pl.ds(f0, FF_BLOCK)], w1buf.at[slot_of(u)], w1_sem.at[slot_of(u)])

    def w2_copy(u):
        e, f0 = expert_of(*loads[u // blocks]), u % blocks * FF_BLOCK
        return pltpu.make_async_copy(w2_hbm.at[e, pl.ds(f0, FF_BLOCK), :], w2buf.at[slot_of(u)], w2_sem.at[slot_of(u)])

    def x_to_pair(k, b):
        src, dst = pl.ds(b * per_exp, per_exp), pl.ds(rows + b * per_exp, per_exp)
        return pltpu.make_async_remote_copy(src_ref=xs.at[expert_of("P", k), src], dst_ref=xpair.at[k, dst], send_sem=xp_send.at[0], recv_sem=xp_recv.at[k], device_id={"data": pair}, device_id_type=MESH)

    def y_to_pair(k):
        return pltpu.make_async_remote_copy(src_ref=yback.at[k], dst_ref=ysall.at[EXPERTS.index(("P", k)), me], send_sem=yb_send.at[0], recv_sem=yb_recv.at[k], device_id={"data": pair}, device_id_type=MESH)

    part = toks // 2
    tok0, tok1 = (Exchange(me, n, lambda half, src, b=b: xall.at[b, src, pl.ds(half * part, part)], lambda pairs, b=b: xall.at[b, pl.ds(0, pairs)], tok_send.at[b], lambda group, b=b: tok_recv.at[b, group], range(6)) for b in range(batch))
    barrier = pltpu.get_barrier_semaphore()
    for peer in (tok0.right, tok0.left, tok0.mate):
        pl.semaphore_signal(barrier, inc=1, device_id={"seq": peer}, device_id_type=MESH)
    pl.semaphore_signal(barrier, inc=1, device_id={"data": pair}, device_id_type=MESH)
    own_in = [pltpu.make_async_copy(tok_hbm.at[b], xall.at[b, me], loc_sem.at[b]) for b in range(batch)]
    for c in own_in:
        c.start()
    phi_in = pltpu.make_async_copy(phi_hbm, phi, loc_sem.at[batch])
    phi_in.start()
    len_in = pltpu.make_async_copy(len_hbm, len_ref, loc_sem.at[batch + 1])
    len_in.start()

    for c in own_in:
        c.wait()
    for u in range(min(ahead, n_loads)):
        w1_copy(u).start()
        w2_copy(u).start()
    pl.semaphore_wait(barrier, 4)
    tok0.own()
    tok1.start(0, 2)

    phi_in.wait()
    len_in.wait()
    d_rows = phi.shape[0]
    n_slots = phi.shape[1]
    step = 64

    def sum_sq(i, acc):
        v = phi[pl.ds(pl.multiple_of(i * step, step), step), :].astype(F32)
        return acc + jnp.sum((v * v).reshape(step // 8, 8, n_slots), axis=0)

    scale = lax.rsqrt(jnp.sum(lax.fori_loop(0, d_rows // step, sum_sq, jnp.zeros((8, n_slots), F32)), axis=0, keepdims=True) + EPSILON)

    def to_unit(i, _):
        at = pl.ds(pl.multiple_of(i * step, step), step)
        phi[at, :] = (phi[at, :].astype(F32) * scale).astype(BF16)
        return 0

    lax.fori_loop(0, d_rows // step, to_unit, 0)
    pnt[...] = phi[:, pl.ds(pl.multiple_of(me * slot_loc, slot_loc), slot_loc)].astype(F32).T.astype(BF16)

    for b in range(batch):
        logits = g * jnp.dot(unit_rows(xall[b, me]), phi[...], preferred_element_type=F32)
        comb = jnp.exp(logits - jnp.max(logits, axis=1, keepdims=True))
        at = pl.ds(b * toks, toks)
        qbuf[at, :] = jnp.broadcast_to(jnp.sum(comb, axis=1, keepdims=True), (toks, 128))
        cbuf[at, :] = comb.astype(BF16)

    tok0.first()
    tok1.start(1, 3, 4, 5)

    def regroup():
        j = lax.broadcasted_iota(jnp.int32, (n_slots, slot_loc), 0)
        k = lax.broadcasted_iota(jnp.int32, (n_slots, slot_loc), 1)
        first = j - ((k // per_exp) * slot_loc + lax.rem(k, per_exp))
        for r, what in enumerate(EXPERTS):
            pick = (first == expert_of(*what) * per_exp).astype(F32).astype(BF16)
            cperm[r] = jnp.dot(cbuf[...], pick, preferred_element_type=F32).astype(BF16)

    regroup()

    def chip_logits(b, src):
        chip = src // 2
        x_chip = xall[b, pl.ds(2 * chip, 2)].reshape(2 * toks, d_model)
        logits = g * lax.dot_general(pnt[...], unit_rows(x_chip), (((1,), (1,)), ((), ())), preferred_element_type=F32)
        pos = chip * (2 * toks) + lax.broadcasted_iota(jnp.int32, logits.shape, 1)
        lt[b, chip] = jnp.where(pos < len_ref[b], logits, NEG_FILL)

    def dispatch(b):
        parts = [lt[b, k] for k in range(chips)]
        top = jnp.max(functools.reduce(jnp.maximum, parts), axis=1, keepdims=True)
        disp = [jnp.exp(p - top) for p in parts]
        col_sum = jnp.sum(functools.reduce(jnp.add, disp), axis=1, keepdims=True)
        weights = jnp.concatenate([w.astype(BF16) for w in disp], axis=1)
        slot_sum = jnp.dot(weights, xall[b].reshape(n * toks, d_model), preferred_element_type=F32)
        at = pl.ds(b * per_exp, per_exp)
        xs[:, at, :] = (slot_sum / col_sum).astype(BF16).reshape(n_exp, per_exp, d_model)
        for k in range(SHARED):
            x_to_pair(k, b).start()
            xpair[k, at] = xs[expert_of("A", k), at]

    tok0.second()
    tok0.arrived(MATE, 1)
    chip_logits(0, me)
    tok1.first()
    tok0.third()
    tok0.arrived(MATE_NEAR, 2)
    chip_logits(0, tok0.left)
    chip_logits(0, tok0.right)
    tok0.arrived(MATE_FAR, 1)
    chip_logits(0, tok0.far)
    dispatch(0)
    yacc[...] = jnp.zeros_like(yacc)

    def ys_ex(r):
        kind, k, only = RINGS[r]
        buf, half_d = EXPERTS.index((kind, k)), d_model // 2

        def chunk(half, src):
            if only is None:
                return ysall.at[buf, src, pl.ds(half * per_exp, per_exp)]
            return ysall.at[buf, src, pl.ds(only * per_exp, per_exp), pl.ds(half * half_d, half_d)]

        def span(pairs):
            if only is None:
                return ysall.at[buf, pl.ds(0, pairs)]
            return ysall.at[buf, pl.ds(0, pairs), pl.ds(only * per_exp, per_exp)]

        return Exchange(me, n, chunk, span, ys_send.at[r], lambda group: ys_recv.at[r, group], (FIRST, SECOND, THIRD, MATE, MATE, MATE))

    def combine(r):
        kind, k, only = RINGS[r]
        buf = EXPERTS.index((kind, k))
        for b in range(batch) if only is None else (only,):
            at = pl.ds(b * toks, toks)
            got = ysall[buf, :, pl.ds(b * per_exp, per_exp), :].reshape(n * per_exp, d_model)
            yacc[at, :] += jnp.dot(cperm[buf, at, :], got, preferred_element_type=F32)

    def run_blocks(todo):
        for b in todo:
            if b < units:
                kind, k, only = job_of(b)
                if kind == "A" and b % blocks == 0:
                    whole = xpair.at[k, pl.ds(rows, rows)]
                    pltpu.make_async_remote_copy(src_ref=whole, dst_ref=whole, send_sem=xp_send.at[0], recv_sem=xp_recv.at[k], device_id={"data": pair}, device_id_type=MESH).wait_recv()
                if not used_before(b):
                    w1_copy(load_of(b)).wait()
            if b > 0 and not used_before(b - 1):
                w2_copy(load_of(b - 1)).wait()
        back = []
        for b in todo:
            if b < units:
                kind, k, only = job_of(b)
                if kind == "A":
                    x_job = xpair[k]
                elif only is None:
                    x_job = xs[expert_of(kind, k)]
                else:
                    x_job = xs[expert_of(kind, k), pl.ds(only * per_exp, per_exp)]
                pre = jnp.dot(x_job, w1buf[slot_of(load_of(b))], preferred_element_type=F32)
            if b > 0:
                kind, k, only = job_of(b - 1)
                live = pl.ds(0, 2 * rows if kind == "A" else rows if only is None else per_exp)
                out = jnp.dot(hidden[(b - 1) % 2, live, :], w2buf[slot_of(load_of(b - 1))], preferred_element_type=F32)
                if (b - 1) % blocks:
                    out = yexp[live, :] + out
                if b % blocks:
                    yexp[live, :] = out
                else:
                    buf = EXPERTS.index((kind, k))
                    if only is None:
                        ysall[buf, me] = out[:rows].astype(BF16)
                    else:
                        ysall[buf, me, pl.ds(only * per_exp, per_exp)] = out.astype(BF16)
                    if kind == "A":
                        yback[k] = out[rows:].astype(BF16)
                        back.append(k)
            if b < units:
                hidden[b % 2, pl.ds(0, pre.shape[0]), :] = jax.nn.gelu(pre).astype(BF16)
        for b in todo:
            if b < units and not used_again(b) and next_load(load_of(b)) is not None:
                w1_copy(next_load(load_of(b))).start()
            if b > 0 and not used_again(b - 1) and next_load(load_of(b - 1)) is not None:
                w2_copy(next_load(load_of(b - 1))).start()
        for k in back:
            y_to_pair(k).start()

    def act(kind, r):
        if kind == "S":
            tok1.second()
        elif kind == "L":
            tok1.arrived(MATE, 1)
            tok1.arrived(MATE_NEAR, 2)
            for src in (me, tok1.left, tok1.right):
                chip_logits(1, src)
        elif kind == "T":
            tok1.third()
        elif kind == "D":
            tok1.arrived(MATE_FAR, 1)
            chip_logits(1, tok1.far)
            dispatch(1)
        elif kind == "o":
            if RINGS[r][0] == "P":
                y_to_pair(RINGS[r][1]).wait_recv()
            ys_ex(r).own()
        elif kind == "f":
            ys_ex(r).first()
        elif kind == "s":
            ys_ex(r).second()
        elif kind == "t":
            ys_ex(r).third()
        else:
            ys_ex(r).arrived(MATE, 4)
            combine(r)

    done = 0
    for what in PROGRAM:
        kind, r = what[0], int(what[1:])
        with jax.named_scope(what if kind != "B" else f"B{done}"):
            if kind == "B":
                run_blocks(range(done, done + r))
                done += r
            else:
                act(kind, r)
    with jax.named_scope("final"):
        for b in range(batch):
            at = pl.ds(b * toks, toks)
            pos = me * toks + lax.broadcasted_iota(jnp.int32, (toks, 1), 0)
            out_ref[b] = jnp.where(pos < len_ref[b], yacc[at, :] / qbuf[at, 0:1], 0.0).astype(BF16)
    with jax.named_scope("sent"):
        for ex in (tok0, tok1, *(ys_ex(r) for r in range(len(RINGS)))):
            ex.sent()
        pltpu.make_async_remote_copy(src_ref=yback, dst_ref=yback, send_sem=xp_send.at[0], recv_sem=xp_recv.at[0], device_id={"data": pair}, device_id_type=MESH).wait_send()
        pltpu.make_async_remote_copy(src_ref=yback, dst_ref=yback, send_sem=yb_send.at[0], recv_sem=yb_recv.at[0], device_id={"data": pair}, device_id_type=MESH).wait_send()


def solution(mesh):
    n = mesh.shape["seq"]

    def local_layer(tok_blk, len_blk, slot_param, logit_scale, w_in, w_out):
        batch, toks, d_model = tok_blk.shape
        n_slots = slot_param.shape[1]
        n_exp = w_in.shape[0]
        slot_loc = n_slots // n
        rows = batch * (slot_loc // n_exp)
        dma = pltpu.SemaphoreType.DMA
        any_spec = pl.BlockSpec(memory_space=pl.ANY)
        smem_spec = pl.BlockSpec(memory_space=pltpu.SMEM)
        return pl.pallas_call(
            functools.partial(kernel, n),
            out_shape=pltpu.VMEM(tok_blk.shape, BF16),
            in_specs=[any_spec, any_spec, any_spec, smem_spec, any_spec, any_spec],
            out_specs=pl.BlockSpec(memory_space=pltpu.VMEM),
            scratch_shapes=[
                pltpu.VMEM((batch, n, toks, d_model), BF16),
                pltpu.VMEM(slot_param.shape, BF16),
                pltpu.VMEM((slot_loc, d_model), BF16),
                pltpu.VMEM((batch, n // 2, slot_loc, 2 * toks), F32),
                pltpu.VMEM((batch * toks, n_slots), BF16),
                pltpu.VMEM((batch * toks, 128), F32),
                pltpu.VMEM((n_exp, batch * toks, n_slots // n_exp), BF16),
                pltpu.VMEM((n_exp, rows, d_model), BF16),
                pltpu.VMEM((SHARED, 2 * rows, d_model), BF16),
                pltpu.VMEM((n_exp, n, rows, d_model), BF16),
                pltpu.VMEM((SHARED, rows, d_model), BF16),
                pltpu.VMEM((2, 2 * rows, FF_BLOCK), BF16),
                pltpu.VMEM((2 * rows, d_model), F32),
                pltpu.VMEM((batch * toks, d_model), F32),
                pltpu.VMEM((AHEAD, d_model, FF_BLOCK), BF16),
                pltpu.VMEM((AHEAD, FF_BLOCK, d_model), BF16),
                dma((batch + 2,)), dma((AHEAD,)), dma((AHEAD,)),
                dma((batch,)), dma((batch, 6)), dma((len(RINGS),)), dma((len(RINGS), 4)),
                dma((1,)), dma((SHARED,)), dma((1,)), dma((SHARED,)),
                pltpu.SMEM((batch,), jnp.int32),
            ],
            compiler_params=pltpu.CompilerParams(collective_id=0, has_side_effects=True, vmem_limit_bytes=VMEM_BYTES),
        )(tok_blk, len_blk, slot_param, logit_scale.reshape(1), w_in, w_out)

    return jax.shard_map(local_layer, mesh=mesh, in_specs=(P("data", "seq", None), P("data"), P(None, None), P(), P("seq", None, None), P("seq", None, None)), out_specs=P("data", "seq", None), check_vma=False)
```

time: 53.9 us -> 50.1 us (0.929)
  Pallas kernels: 52.4 us -> 48.6 us
    pallas_call x1, Pallas kernels: 52.4 us -> 48.6 us  [local_layer(): pl.pallas_call(functools.partial(kernel, n), out_shape=pltpu.VMEM(tok_blk...]
where the time goes in v3:
time: 50.1 us; the launch traced here: 50 us
  Pallas kernels  48.6 us (97%)
  local copies, waits for them, and re-layouts  0.71 us (1%)
  between operations  0.66 us (1%)
    pallas_call x1, Pallas kernels, local_layer(): pl.pallas_call(functools.partial(kernel, n), out_shape=pltpu.VMEM(tok_blk...  48.6 us

profile of v3, /device:TPU:113, one launch (start us, length us, event | category | flops | bytes accessed | tf_op | source)
XLA Modules:
  0.0 50.0 jit_solution(17443479054755053157)
XLA Ops:
  0.7 48.6 %shard_map.64 = bf16[2,64,1024]{2,1,0:T(8,128)(2,1)S(1)} custom-call(bf16[2,64,1024]{2,1,0:T(8,128)(2,1)} %tok_hbm.1, s32[2]{0:T(128)} %len_hbm.1, bf16[1024,1024]{1,0:T(8,128)(2,1)} %phi_hbm.1, f32[1]{0:T(128)} %bitcast.1.g_ref, bf16[8,1024,4096]{2,1,0:T(8,128)(2,1)} %w1_hbm.1, bf16[8,4096,1024]{2,1,0:T(8,128)(2,1)} %w2_hbm.1), custom_call_target="tpu_custom_call" | custom-call | tf_op jit(solution)/shard_map/pallas_call | solution.py:369
  49.3 0.7 %copy.8 = bf16[2,64,1024]{2,1,0:T(8,128)(2,1)} copy(bf16[2,64,1024]{2,1,0:T(8,128)(2,1)S(1)} %shard_map.64) | data formatting | bytes 524288

commit v4 on v3

--- a/solution.py
+++ b/solution.py
@@ -17,11 +17,12 @@
 EXPERTS = (("U", 0), ("A", 0), ("A", 1), ("P", 0), ("A", 2), ("P", 1), ("U", 1), ("P", 2))
 RINGS = (("U", 0, 0), ("U", 1, None), ("A", 0, None), ("A", 1, None), ("P", 0, None), ("A", 2, None), ("P", 1, None), ("U", 0, 1), ("P", 2, None))
 BEFORE, SHARED = 1, 3
+DIRECT = (7,)
 PROGRAM = (
-    "B2", "S1", "B1", "T1", "B1", "L1", "D1", "B1", "o0", "B1", "B1", "B1", "B1", "f0", "s0", "o1", "B1", "B1", "B1", "B1", "t0", "o2",
-    "B1", "f1", "B1", "m0", "s1", "B1", "B1", "o3", "f2", "B1", "o4", "s2", "B1", "t1", "B1", "B1", "o5", "m1", "f3", "B1", "o6", "s3",
-    "B2", "t2", "B1", "f4", "o7", "s4", "t3", "o8", "f5", "s5", "m2", "f6", "s6", "t4", "f7", "s7", "m3", "f8", "s8", "t5", "t6", "m4",
-    "t7", "t8", "m5", "m6", "m7", "m8",
+    "S1", "B2", "L1", "T1", "B1", "D1", "B1", "B1", "o0", "B1", "B1", "B1", "F1", "o1", "B1", "B1", "f0", "s0", "B1", "B1", "F1", "o2",
+    "B1", "f1", "B1", "s1", "B1", "t0", "B1", "B1", "o3", "m0", "B1", "f2", "f4", "B1", "B1", "s2", "s4", "B1", "t1", "o5", "B1", "B1",
+    "B1", "f3", "f6", "m1", "F1", "o7", "s3", "s6", "t2", "o4", "t4", "o6", "f5", "f8", "s5", "s8", "t3", "o8", "m2", "t6", "f7", "s7",
+    "m4", "t5", "t7", "t8", "m3", "m6", "m5", "m7", "m8",
 )
 AHEAD = 12
 VMEM_BYTES = 62 * 1024 * 1024
@@ -36,17 +37,18 @@
 
 
 class Exchange:
-    def __init__(self, me, n, chunk, span, send_sem, recv_sem, groups):
+    def __init__(self, me, n, chunk, span, send_sem, recv_sem, groups, direct=False):
         core = lax.rem(me, 2)
         self.me, self.mate = me, me + 1 - 2 * core
         self.right, self.left = lax.rem(me + 2, n), lax.rem(me + n - 2, n)
         self.far = lax.rem(me + n // 2, n)
-        self.chunk, self.span, self.send_sem, self.recv_sem, self.groups = chunk, span, send_sem, recv_sem, groups
+        self.chunk, self.span, self.send_sem, self.recv_sem, self.groups, self.direct = chunk, span, send_sem, recv_sem, groups, direct
 
     def plan(self):
         me, right, left, far, mate = self.me, self.right, self.left, self.far, self.mate
+        onward = [(0, me, far, THIRD), (1, me, far, THIRD)] if self.direct else [(0, left, right, THIRD), (1, right, left, THIRD)]
         return [(0, me, right, FIRST), (1, me, right, SECOND), (1, me, left, FIRST), (0, me, left, SECOND), (0, me, mate, MATE), (1, me, mate, MATE),
-                (0, left, right, THIRD), (1, right, left, THIRD), (0, left, mate, MATE_NEAR), (1, right, mate, MATE_NEAR),
+                *onward, (0, left, mate, MATE_NEAR), (1, right, mate, MATE_NEAR),
                 (1, left, mate, MATE_NEAR), (0, right, mate, MATE_NEAR), (0, far, mate, MATE_FAR), (1, far, mate, MATE_FAR)]
 
     def start(self, *which):
@@ -59,11 +61,11 @@
         pltpu.make_async_remote_copy(src_ref=ref, dst_ref=ref, send_sem=self.send_sem, recv_sem=self.recv_sem(group), device_id={"seq": self.mate}, device_id_type=MESH).wait_recv()
 
     def own(self):
-        self.start(0, 1, 2, 3, 4, 5)
+        self.start(0, 1, 2, 3, 4, 5, *((6, 7) if self.direct else ()))
 
     def first(self):
         self.arrived(FIRST, 1)
-        self.start(6, 7, 8, 9)
+        self.start(*(() if self.direct else (6, 7)), 8, 9)
 
     def second(self):
         self.arrived(SECOND, 1)
@@ -73,13 +75,13 @@
         self.arrived(THIRD, 1)
         self.start(12, 13)
 
-    def sent(self):
-        ref = self.span(7)
+    def sent(self, pairs=7):
+        ref = self.span(pairs)
         pltpu.make_async_remote_copy(src_ref=ref, dst_ref=ref, send_sem=self.send_sem, recv_sem=self.recv_sem(0), device_id={"seq": self.mate}, device_id_type=MESH).wait_send()
 
 
 def kernel(n, tok_hbm, len_hbm, phi_hbm, g_ref, w1_hbm, w2_hbm, out_ref, xall, phi, pnt, lt, cbuf, qbuf, cperm, xs, xpair, ysall, yback, hidden, yexp, yacc, w1buf, w2buf,
-           loc_sem, w1_sem, w2_sem, tok_send, tok_recv, ys_send, ys_recv, xp_send, xp_recv, yb_send, yb_recv, len_ref):
+           loc_sem, w1_sem, w2_sem, tok_send, tok_recv, ys_send, ys_recv, xp_send, xp_recv, yb_send, yb_recv, len_ref, pairs_in):
     batch, _, toks, d_model = xall.shape
     n_exp, _, rows, _ = ysall.shape
     per_exp = rows // batch
@@ -99,42 +101,30 @@
             return k if k < BEFORE else k + 2 * SHARED
         return BEFORE + SHARED * (odd if kind == "A" else 1 - odd) + k
 
-    loads = list(dict.fromkeys((kind, k) for kind, k, _ in JOBS))
-    n_loads = len(loads) * blocks
     units = len(JOBS) * blocks
 
     def job_of(b):
         return JOBS[b // blocks]
 
-    def load_of(b):
-        return loads.index(job_of(b)[:2]) * blocks + b % blocks
-
-    def used_again(b):
-        return any(load_of(later) == load_of(b) for later in range(b + 1, units))
-
-    def used_before(b):
-        return any(load_of(early) == load_of(b) for early in range(b))
-
-    def slot_of(u):
-        return u if u < ahead else blocks + (u - ahead) % (ahead - blocks)
-
-    def next_load(u):
-        return next((v for v in range(u + 1, n_loads) if slot_of(v) == slot_of(u)), None)
-
-    def w1_copy(u):
-        e, f0 = expert_of(*loads[u // blocks]), u % blocks * FF_BLOCK
-        return pltpu.make_async_copy(w1_hbm.at[e, :, pl.ds(f0, FF_BLOCK)], w1buf.at[slot_of(u)], w1_sem.at[slot_of(u)])
-
-    def w2_copy(u):
-        e, f0 = expert_of(*loads[u // blocks]), u % blocks * FF_BLOCK
-        return pltpu.make_async_copy(w2_hbm.at[e, pl.ds(f0, FF_BLOCK), :], w2buf.at[slot_of(u)], w2_sem.at[slot_of(u)])
+    def w1_copy(b):
+        e, f0 = expert_of(*job_of(b)[:2]), b % blocks * FF_BLOCK
+        return pltpu.make_async_copy(w1_hbm.at[e, :, pl.ds(f0, FF_BLOCK)], w1buf.at[b % ahead], w1_sem.at[b % ahead])
+
+    def w2_copy(b):
+        e, f0 = expert_of(*job_of(b)[:2]), b % blocks * FF_BLOCK
+        return pltpu.make_async_copy(w2_hbm.at[e, pl.ds(f0, FF_BLOCK), :], w2buf.at[b % ahead], w2_sem.at[b % ahead])
 
     def x_to_pair(k, b):
         src, dst = pl.ds(b * per_exp, per_exp), pl.ds(rows + b * per_exp, per_exp)
         return pltpu.make_async_remote_copy(src_ref=xs.at[expert_of("P", k), src], dst_ref=xpair.at[k, dst], send_sem=xp_send.at[0], recv_sem=xp_recv.at[k], device_id={"data": pair}, device_id_type=MESH)
 
-    def y_to_pair(k):
-        return pltpu.make_async_remote_copy(src_ref=yback.at[k], dst_ref=ysall.at[EXPERTS.index(("P", k)), me], send_sem=yb_send.at[0], recv_sem=yb_recv.at[k], device_id={"data": pair}, device_id_type=MESH)
+    def y_to_pair(k, *which):
+        buf = EXPERTS.index(("P", k))
+        r = RINGS.index(("P", k, None))
+        plan = ((0, tok0.right, ys_recv.at[r, FIRST]), (1, tok0.left, ys_recv.at[r, FIRST]), (1, tok0.right, ys_recv.at[r, SECOND]), (0, tok0.left, ys_recv.at[r, SECOND]), (0, me, yb_recv.at[k]), (1, me, yb_recv.at[k]))
+        for half, to, sem in (plan[i] for i in which):
+            at = pl.ds(half * per_exp, per_exp)
+            pltpu.make_async_remote_copy(src_ref=yback.at[k, at], dst_ref=ysall.at[buf, me, at], send_sem=yb_send.at[0], recv_sem=sem, device_id={"data": pair, "seq": to}, device_id_type=MESH).start()
 
     part = toks // 2
     tok0, tok1 = (Exchange(me, n, lambda half, src, b=b: xall.at[b, src, pl.ds(half * part, part)], lambda pairs, b=b: xall.at[b, pl.ds(0, pairs)], tok_send.at[b], lambda group, b=b: tok_recv.at[b, group], range(6)) for b in range(batch))
@@ -152,12 +142,14 @@
 
     for c in own_in:
         c.wait()
-    for u in range(min(ahead, n_loads)):
+    for u in range(min(ahead, units)):
         w1_copy(u).start()
         w2_copy(u).start()
     pl.semaphore_wait(barrier, 4)
     tok0.own()
     tok1.start(0, 2)
+    for peer in (tok0.right, tok0.left):
+        pl.semaphore_signal(pairs_in, inc=1, device_id={"seq": peer}, device_id_type=MESH)
 
     phi_in.wait()
     len_in.wait()
@@ -227,9 +219,17 @@
     tok0.arrived(MATE_NEAR, 2)
     chip_logits(0, tok0.left)
     chip_logits(0, tok0.right)
+    upper = lax.rem(me, 2) == 1
+
+    @pl.when(upper)
+    def _():
+        tok1.second()
+        tok1.third()
+
     tok0.arrived(MATE_FAR, 1)
     chip_logits(0, tok0.far)
     dispatch(0)
+    pl.semaphore_wait(pairs_in, 2)
     yacc[...] = jnp.zeros_like(yacc)
 
     def ys_ex(r):
@@ -246,7 +246,7 @@
                 return ysall.at[buf, pl.ds(0, pairs)]
             return ysall.at[buf, pl.ds(0, pairs), pl.ds(only * per_exp, per_exp)]
 
-        return Exchange(me, n, chunk, span, ys_send.at[r], lambda group: ys_recv.at[r, group], (FIRST, SECOND, THIRD, MATE, MATE, MATE))
+        return Exchange(me, n, chunk, span, ys_send.at[r], lambda group: ys_recv.at[r, group], (FIRST, SECOND, THIRD, MATE, MATE, MATE), r in DIRECT)
 
     def combine(r):
         kind, k, only = RINGS[r]
@@ -256,20 +256,34 @@
             got = ysall[buf, :, pl.ds(b * per_exp, per_exp), :].reshape(n * per_exp, d_model)
             yacc[at, :] += jnp.dot(cperm[buf, at, :], got, preferred_element_type=F32)
 
-    def run_blocks(todo):
-        for b in todo:
-            if b < units:
-                kind, k, only = job_of(b)
-                if kind == "A" and b % blocks == 0:
-                    whole = xpair.at[k, pl.ds(rows, rows)]
-                    pltpu.make_async_remote_copy(src_ref=whole, dst_ref=whole, send_sem=xp_send.at[0], recv_sem=xp_recv.at[k], device_id={"data": pair}, device_id_type=MESH).wait_recv()
-                if not used_before(b):
-                    w1_copy(load_of(b)).wait()
-            if b > 0 and not used_before(b - 1):
-                w2_copy(load_of(b - 1)).wait()
-        back = []
-        for b in todo:
-            if b < units:
+    def second_matmul(b):
+        kind, k, only = job_of(b)
+        live = pl.ds(0, 2 * rows if kind == "A" else rows if only is None else per_exp)
+        out = jnp.dot(hidden[b % 2, live, :], w2buf[b % ahead], preferred_element_type=F32)
+        if b % blocks:
+            out = yexp[live, :] + out
+        if (b + 1) % blocks:
+            yexp[live, :] = out
+            return
+        buf = EXPERTS.index((kind, k))
+        if only is None:
+            ysall[buf, me] = out[:rows].astype(BF16)
+        else:
+            ysall[buf, me, pl.ds(only * per_exp, per_exp)] = out.astype(BF16)
+        if kind == "A":
+            yback[k] = out[rows:].astype(BF16)
+
+    def run(firsts, seconds):
+        for b in firsts:
+            kind, k, only = job_of(b)
+            if kind == "A" and b % blocks == 0:
+                whole = xpair.at[k, pl.ds(rows, rows)]
+                pltpu.make_async_remote_copy(src_ref=whole, dst_ref=whole, send_sem=xp_send.at[0], recv_sem=xp_recv.at[k], device_id={"data": pair}, device_id_type=MESH).wait_recv()
+            w1_copy(b).wait()
+        for b in seconds:
+            w2_copy(b).wait()
+        for b in sorted({*firsts, *(b + 1 for b in seconds)}):
+            if b in firsts:
                 kind, k, only = job_of(b)
                 if kind == "A":
                     x_job = xpair[k]
@@ -277,52 +291,45 @@
                     x_job = xs[expert_of(kind, k)]
                 else:
                     x_job = xs[expert_of(kind, k), pl.ds(only * per_exp, per_exp)]
-                pre = jnp.dot(x_job, w1buf[slot_of(load_of(b))], preferred_element_type=F32)
-            if b > 0:
-                kind, k, only = job_of(b - 1)
-                live = pl.ds(0, 2 * rows if kind == "A" else rows if only is None else per_exp)
-                out = jnp.dot(hidden[(b - 1) % 2, live, :], w2buf[slot_of(load_of(b - 1))], preferred_element_type=F32)
-                if (b - 1) % blocks:
-                    out = yexp[live, :] + out
-                if b % blocks:
-                    yexp[live, :] = out
-                else:
-                    buf = EXPERTS.index((kind, k))
-                    if only is None:
-                        ysall[buf, me] = out[:rows].astype(BF16)
-                    else:
-                        ysall[buf, me, pl.ds(only * per_exp, per_exp)] = out.astype(BF16)
-                    if kind == "A":
-                        yback[k] = out[rows:].astype(BF16)
-                        back.append(k)
-            if b < units:
+                pre = jnp.dot(x_job, w1buf[b % ahead], preferred_element_type=F32)
+            if b - 1 in seconds:
+                second_matmul(b - 1)
+            if b in firsts:
                 hidden[b % 2, pl.ds(0, pre.shape[0]), :] = jax.nn.gelu(pre).astype(BF16)
-        for b in todo:
-            if b < units and not used_again(b) and next_load(load_of(b)) is not None:
-                w1_copy(next_load(load_of(b))).start()
-            if b > 0 and not used_again(b - 1) and next_load(load_of(b - 1)) is not None:
-                w2_copy(next_load(load_of(b - 1))).start()
-        for k in back:
-            y_to_pair(k).start()
+        for b in firsts:
+            if b + ahead < units:
+                w1_copy(b + ahead).start()
+        for b in seconds:
+            if b + ahead < units:
+                w2_copy(b + ahead).start()
 
     def act(kind, r):
         if kind == "S":
-            tok1.second()
+            pl.when(jnp.logical_not(upper))(tok1.second)
         elif kind == "L":
             tok1.arrived(MATE, 1)
             tok1.arrived(MATE_NEAR, 2)
             for src in (me, tok1.left, tok1.right):
                 chip_logits(1, src)
         elif kind == "T":
-            tok1.third()
+            pl.when(jnp.logical_not(upper))(tok1.third)
         elif kind == "D":
             tok1.arrived(MATE_FAR, 1)
             chip_logits(1, tok1.far)
             dispatch(1)
         elif kind == "o":
             if RINGS[r][0] == "P":
-                y_to_pair(RINGS[r][1]).wait_recv()
-            ys_ex(r).own()
+                mine = yback.at[RINGS[r][1]]
+                pltpu.make_async_remote_copy(src_ref=mine, dst_ref=mine, send_sem=yb_send.at[0], recv_sem=yb_recv.at[RINGS[r][1]], device_id={"data": pair}, device_id_type=MESH).wait_recv()
+                ys_ex(r).start(4, 5)
+            elif RINGS[r][0] == "A":
+                y_to_pair(RINGS[r][1], 0, 1)
+                ys_ex(r).start(0, 2)
+                y_to_pair(RINGS[r][1], 2, 3)
+                ys_ex(r).start(1, 3, 4, 5)
+                y_to_pair(RINGS[r][1], 4, 5)
+            else:
+                ys_ex(r).own()
         elif kind == "f":
             ys_ex(r).first()
         elif kind == "s":
@@ -333,25 +340,33 @@
             ys_ex(r).arrived(MATE, 4)
             combine(r)
 
-    done = 0
+    firsts = seconds = 0
     for what in PROGRAM:
         kind, r = what[0], int(what[1:])
-        with jax.named_scope(what if kind != "B" else f"B{done}"):
+        with jax.named_scope(what if kind not in "BF" else f"{kind}{firsts}"):
             if kind == "B":
-                run_blocks(range(done, done + r))
-                done += r
+                run(range(firsts, firsts + r), range(seconds, firsts + r - 1))
+                firsts, seconds = firsts + r, firsts + r - 1
+            elif kind == "F":
+                run((), (seconds,))
+                seconds += 1
             else:
                 act(kind, r)
+    assert seconds == units
+
     with jax.named_scope("final"):
         for b in range(batch):
             at = pl.ds(b * toks, toks)
             pos = me * toks + lax.broadcasted_iota(jnp.int32, (toks, 1), 0)
             out_ref[b] = jnp.where(pos < len_ref[b], yacc[at, :] / qbuf[at, 0:1], 0.0).astype(BF16)
     with jax.named_scope("sent"):
-        for ex in (tok0, tok1, *(ys_ex(r) for r in range(len(RINGS)))):
-            ex.sent()
+        tok0.sent()
+        tok1.sent()
+        for r in range(len(RINGS)):
+            ys_ex(r).sent(5 if RINGS[r][0] == "P" else 7)
         pltpu.make_async_remote_copy(src_ref=yback, dst_ref=yback, send_sem=xp_send.at[0], recv_sem=xp_recv.at[0], device_id={"data": pair}, device_id_type=MESH).wait_send()
-        pltpu.make_async_remote_copy(src_ref=yback, dst_ref=yback, send_sem=yb_send.at[0], recv_sem=yb_recv.at[0], device_id={"data": pair}, device_id_type=MESH).wait_send()
+        given = ysall.at[pl.ds(0, SHARED), pl.ds(0, 3)]
+        pltpu.make_async_remote_copy(src_ref=given, dst_ref=given, send_sem=yb_send.at[0], recv_sem=yb_recv.at[0], device_id={"data": pair}, device_id_type=MESH).wait_send()
 
 
 def solution(mesh):
@@ -392,6 +407,7 @@
                 dma((batch,)), dma((batch, 6)), dma((len(RINGS),)), dma((len(RINGS), 4)),
                 dma((1,)), dma((SHARED,)), dma((1,)), dma((SHARED,)),
                 pltpu.SMEM((batch,), jnp.int32),
+                pltpu.SemaphoreType.REGULAR,
             ],
             compiler_params=pltpu.CompilerParams(collective_id=0, has_side_effects=True, vmem_limit_bytes=VMEM_BYTES),
         )(tok_blk, len_blk, slot_param, logit_scale.reshape(1), w_in, w_out)

time: 50.1 us -> 47.6 us (0.950)
  Pallas kernels: 48.6 us -> 46.1 us
    pallas_call x1, Pallas kernels: 48.6 us -> 46.1 us  [local_layer(): pl.pallas_call(functools.partial(kernel, n), out_shape=pltpu.VMEM(tok_blk...]
where the time goes in v4:
time: 47.6 us; the launch traced here: 47.5 us
  Pallas kernels  46.1 us (97%)
  local copies, waits for them, and re-layouts  0.71 us (1%)
  between operations  0.66 us (1%)
    pallas_call x1, Pallas kernels, local_layer(): pl.pallas_call(functools.partial(kernel, n), out_shape=pltpu.VMEM(tok_blk...  46.1 us

profile of v4, /device:TPU:113, one launch (start us, length us, event | category | flops | bytes accessed | tf_op | source)
XLA Modules:
  0.0 47.5 jit_solution(9859141411688282518)
XLA Ops:
  0.7 46.1 %shard_map.64 = bf16[2,64,1024]{2,1,0:T(8,128)(2,1)S(1)} custom-call(bf16[2,64,1024]{2,1,0:T(8,128)(2,1)} %tok_hbm.1, s32[2]{0:T(128)} %len_hbm.1, bf16[1024,1024]{1,0:T(8,128)(2,1)} %phi_hbm.1, f32[1]{0:T(128)} %bitcast.1.g_ref, bf16[8,1024,4096]{2,1,0:T(8,128)(2,1)} %w1_hbm.1, bf16[8,4096,1024]{2,1,0:T(8,128)(2,1)} %w2_hbm.1), custom_call_target="tpu_custom_call" | custom-call | tf_op jit(solution)/shard_map/pallas_call | solution.py:384
  46.8 0.7 %copy.8 = bf16[2,64,1024]{2,1,0:T(8,128)(2,1)} copy(bf16[2,64,1024]{2,1,0:T(8,128)(2,1)S(1)} %shard_map.64) | data formatting | bytes 524288

commit v5 on v4

--- a/solution.py
+++ b/solution.py
@@ -17,11 +17,11 @@
 EXPERTS = (("U", 0), ("A", 0), ("A", 1), ("P", 0), ("A", 2), ("P", 1), ("U", 1), ("P", 2))
 RINGS = (("U", 0, 0), ("U", 1, None), ("A", 0, None), ("A", 1, None), ("P", 0, None), ("A", 2, None), ("P", 1, None), ("U", 0, 1), ("P", 2, None))
 BEFORE, SHARED = 1, 3
-DIRECT = (7,)
+DIRECT = (0, 1, 7)
 PROGRAM = (
-    "S1", "B2", "L1", "T1", "B1", "D1", "B1", "B1", "o0", "B1", "B1", "B1", "F1", "o1", "B1", "B1", "f0", "s0", "B1", "B1", "F1", "o2",
-    "B1", "f1", "B1", "s1", "B1", "t0", "B1", "B1", "o3", "m0", "B1", "f2", "f4", "B1", "B1", "s2", "s4", "B1", "t1", "o5", "B1", "B1",
-    "B1", "f3", "f6", "m1", "F1", "o7", "s3", "s6", "t2", "o4", "t4", "o6", "f5", "f8", "s5", "s8", "t3", "o8", "m2", "t6", "f7", "s7",
+    "B2", "S1", "L1", "B1", "T1", "D1", "B1", "B1", "o0", "B1", "B1", "B1", "F1", "o1", "B1", "B1", "B1", "f0", "s0", "B1", "B1", "o2",
+    "t0", "f1", "B1", "B1", "B1", "F1", "o3", "s1", "t1", "m0", "B1", "B1", "f2", "f4", "B1", "m1", "B1", "s2", "s4", "B1", "o5", "B1",
+    "B1", "B1", "f3", "f6", "F1", "o7", "s3", "s6", "t2", "o4", "t4", "f5", "f8", "s5", "s8", "t3", "o6", "m2", "t6", "f7", "s7", "o8",
     "m4", "t5", "t7", "t8", "m3", "m6", "m5", "m7", "m8",
 )
 AHEAD = 12
@@ -75,8 +75,8 @@
         self.arrived(THIRD, 1)
         self.start(12, 13)
 
-    def sent(self, pairs=7):
-        ref = self.span(pairs)
+    def sent(self):
+        ref = self.span(7)
         pltpu.make_async_remote_copy(src_ref=ref, dst_ref=ref, send_sem=self.send_sem, recv_sem=self.recv_sem(0), device_id={"seq": self.mate}, device_id_type=MESH).wait_send()
 
 
@@ -215,10 +215,10 @@
     tok0.arrived(MATE, 1)
     chip_logits(0, me)
     tok1.first()
-    tok0.third()
     tok0.arrived(MATE_NEAR, 2)
     chip_logits(0, tok0.left)
     chip_logits(0, tok0.right)
+    tok0.third()
     upper = lax.rem(me, 2) == 1
 
     @pl.when(upper)
@@ -246,7 +246,7 @@
                 return ysall.at[buf, pl.ds(0, pairs)]
             return ysall.at[buf, pl.ds(0, pairs), pl.ds(only * per_exp, per_exp)]
 
-        return Exchange(me, n, chunk, span, ys_send.at[r], lambda group: ys_recv.at[r, group], (FIRST, SECOND, THIRD, MATE, MATE, MATE), r in DIRECT)
+        return Exchange(me, n, chunk, span, ys_send.at[0 if only is not None else 1 if kind == "P" else 2], lambda group: ys_recv.at[r, group], (FIRST, SECOND, THIRD, MATE, MATE, MATE), r in DIRECT)
 
     def combine(r):
         kind, k, only = RINGS[r]
@@ -325,9 +325,8 @@
             elif RINGS[r][0] == "A":
                 y_to_pair(RINGS[r][1], 0, 1)
                 ys_ex(r).start(0, 2)
-                y_to_pair(RINGS[r][1], 2, 3)
+                y_to_pair(RINGS[r][1], 4, 5, 2, 3)
                 ys_ex(r).start(1, 3, 4, 5)
-                y_to_pair(RINGS[r][1], 4, 5)
             else:
                 ys_ex(r).own()
         elif kind == "f":
@@ -362,8 +361,10 @@
     with jax.named_scope("sent"):
         tok0.sent()
         tok1.sent()
-        for r in range(len(RINGS)):
-            ys_ex(r).sent(5 if RINGS[r][0] == "P" else 7)
+        halves = [ring for ring in RINGS if ring[2] is not None]
+        sent_spans = (ysall.at[pl.ds(0, len(halves)), pl.ds(0, 7), pl.ds(0, per_exp)], ysall.at[pl.ds(0, SHARED), pl.ds(0, 5)], ysall.at[pl.ds(0, len(RINGS) - len(halves) - SHARED), pl.ds(0, 7)])
+        for i, ref in enumerate(sent_spans):
+            pltpu.make_async_remote_copy(src_ref=ref, dst_ref=ref, send_sem=ys_send.at[i], recv_sem=ys_recv.at[0, 0], device_id={"data": pair}, device_id_type=MESH).wait_send()
         pltpu.make_async_remote_copy(src_ref=yback, dst_ref=yback, send_sem=xp_send.at[0], recv_sem=xp_recv.at[0], device_id={"data": pair}, device_id_type=MESH).wait_send()
         given = ysall.at[pl.ds(0, SHARED), pl.ds(0, 3)]
         pltpu.make_async_remote_copy(src_ref=given, dst_ref=given, send_sem=yb_send.at[0], recv_sem=yb_recv.at[0], device_id={"data": pair}, device_id_type=MESH).wait_send()
@@ -404,7 +405,7 @@
                 pltpu.VMEM((AHEAD, d_model, FF_BLOCK), BF16),
                 pltpu.VMEM((AHEAD, FF_BLOCK, d_model), BF16),
                 dma((batch + 2,)), dma((AHEAD,)), dma((AHEAD,)),
-                dma((batch,)), dma((batch, 6)), dma((len(RINGS),)), dma((len(RINGS), 4)),
+                dma((batch,)), dma((batch, 6)), dma((3,)), dma((len(RINGS), 4)),
                 dma((1,)), dma((SHARED,)), dma((1,)), dma((SHARED,)),
                 pltpu.SMEM((batch,), jnp.int32),
                 pltpu.SemaphoreType.REGULAR,

time: 47.6 us -> 46.2 us (0.971)
  Pallas kernels: 46.1 us -> 44.8 us
    pallas_call x1, Pallas kernels: 46.1 us -> 44.8 us  [local_layer(): pl.pallas_call(functools.partial(kernel, n), out_shape=pltpu.VMEM(tok_blk...]
where the time goes in v5:
time: 46.2 us; the launch traced here: 46.1 us
  Pallas kernels  44.8 us (97%)
  local copies, waits for them, and re-layouts  0.71 us (2%)
  between operations  0.66 us (1%)
    pallas_call x1, Pallas kernels, local_layer(): pl.pallas_call(functools.partial(kernel, n), out_shape=pltpu.VMEM(tok_blk...  44.8 us

profile of v5, /device:TPU:113, one launch (start us, length us, event | category | flops | bytes accessed | tf_op | source)
XLA Modules:
  0.0 46.1 jit_solution(17834530350378161163)
XLA Ops:
  0.7 44.8 %shard_map.64 = bf16[2,64,1024]{2,1,0:T(8,128)(2,1)S(1)} custom-call(bf16[2,64,1024]{2,1,0:T(8,128)(2,1)} %tok_hbm.1, s32[2]{0:T(128)} %len_hbm.1, bf16[1024,1024]{1,0:T(8,128)(2,1)} %phi_hbm.1, f32[1]{0:T(128)} %bitcast.1.g_ref, bf16[8,1024,4096]{2,1,0:T(8,128)(2,1)} %w1_hbm.1, bf16[8,4096,1024]{2,1,0:T(8,128)(2,1)} %w2_hbm.1), custom_call_target="tpu_custom_call" | custom-call | tf_op jit(solution)/shard_map/pallas_call | solution.py:385
  45.4 0.7 %copy.8 = bf16[2,64,1024]{2,1,0:T(8,128)(2,1)} copy(bf16[2,64,1024]{2,1,0:T(8,128)(2,1)S(1)} %shard_map.64) | data formatting | bytes 524288

commit v6 on v5

--- a/solution.py
+++ b/solution.py
@@ -19,10 +19,10 @@
 BEFORE, SHARED = 1, 3
 DIRECT = (0, 1, 7)
 PROGRAM = (
-    "B2", "S1", "L1", "B1", "T1", "D1", "B1", "B1", "o0", "B1", "B1", "B1", "F1", "o1", "B1", "B1", "B1", "f0", "s0", "B1", "B1", "o2",
-    "t0", "f1", "B1", "B1", "B1", "F1", "o3", "s1", "t1", "m0", "B1", "B1", "f2", "f4", "B1", "m1", "B1", "s2", "s4", "B1", "o5", "B1",
-    "B1", "B1", "f3", "f6", "F1", "o7", "s3", "s6", "t2", "o4", "t4", "f5", "f8", "s5", "s8", "t3", "o6", "m2", "t6", "f7", "s7", "o8",
-    "m4", "t5", "t7", "t8", "m3", "m6", "m5", "m7", "m8",
+    "B2", "S1", "L1", "B1", "T1", "D1", "B1", "B1", "o0", "B1", "B1", "B1", "B1", "o1", "B1", "B1", "f0", "s0", "B1", "B1", "o2", "t0",
+    "f1", "B1", "B1", "G1", "o3", "s1", "t1", "m0", "B1", "B1", "f2", "f4", "B1", "m1", "B1", "s2", "s4", "B1", "o5", "B1", "B1", "B1",
+    "f3", "f6", "F1", "o7", "s3", "s6", "t2", "o4", "t4", "f5", "f8", "s5", "s8", "t3", "o6", "m2", "t6", "f7", "s7", "o8", "m4", "t5",
+    "t7", "t8", "m3", "m6", "m5", "m7", "m8",
 )
 AHEAD = 12
 VMEM_BYTES = 62 * 1024 * 1024
@@ -342,13 +342,16 @@
     firsts = seconds = 0
     for what in PROGRAM:
         kind, r = what[0], int(what[1:])
-        with jax.named_scope(what if kind not in "BF" else f"{kind}{firsts}"):
+        with jax.named_scope(what if kind not in "BFG" else f"{kind}{firsts}"):
             if kind == "B":
                 run(range(firsts, firsts + r), range(seconds, firsts + r - 1))
                 firsts, seconds = firsts + r, firsts + r - 1
             elif kind == "F":
                 run((), (seconds,))
                 seconds += 1
+            elif kind == "G":
+                run(range(firsts, firsts + r), range(seconds, firsts + r))
+                firsts = seconds = firsts + r
             else:
                 act(kind, r)
     assert seconds == units

time: 46.2 us -> 46.1 us (level)
  no operation moved by 1% of the time
where the time goes in v6:
time: 46.1 us; the launch traced here: 46 us
  Pallas kernels  44.6 us (97%)
  local copies, waits for them, and re-layouts  0.71 us (2%)
  between operations  0.66 us (1%)
    pallas_call x1, Pallas kernels, local_layer(): pl.pallas_call(functools.partial(kernel, n), out_shape=pltpu.VMEM(tok_blk...  44.6 us

profile of v6, /device:TPU:113, one launch (start us, length us, event | category | flops | bytes accessed | tf_op | source)
XLA Modules:
  0.0 46.0 jit_solution(6529326705128110709)
XLA Ops:
  0.7 44.6 %shard_map.64 = bf16[2,64,1024]{2,1,0:T(8,128)(2,1)S(1)} custom-call(bf16[2,64,1024]{2,1,0:T(8,128)(2,1)} %tok_hbm.1, s32[2]{0:T(128)} %len_hbm.1, bf16[1024,1024]{1,0:T(8,128)(2,1)} %phi_hbm.1, f32[1]{0:T(128)} %bitcast.1.g_ref, bf16[8,1024,4096]{2,1,0:T(8,128)(2,1)} %w1_hbm.1, bf16[8,4096,1024]{2,1,0:T(8,128)(2,1)} %w2_hbm.1), custom_call_target="tpu_custom_call" | custom-call | tf_op jit(solution)/shard_map/pallas_call | solution.py:388
  45.3 0.7 %copy.8 = bf16[2,64,1024]{2,1,0:T(8,128)(2,1)} copy(bf16[2,64,1024]{2,1,0:T(8,128)(2,1)S(1)} %shard_map.64) | data formatting | bytes 524288

commit v7 on v6

--- a/solution.py
+++ b/solution.py
@@ -81,7 +81,7 @@
 
 
 def kernel(n, tok_hbm, len_hbm, phi_hbm, g_ref, w1_hbm, w2_hbm, out_ref, xall, phi, pnt, lt, cbuf, qbuf, cperm, xs, xpair, ysall, yback, hidden, yexp, yacc, w1buf, w2buf,
-           loc_sem, w1_sem, w2_sem, tok_send, tok_recv, ys_send, ys_recv, xp_send, xp_recv, yb_send, yb_recv, len_ref, pairs_in):
+           loc_sem, w_sem, tok_send, tok_recv, ys_send, ys_recv, xp_send, xp_recv, yb_send, yb_recv, len_ref, pairs_in):
     batch, _, toks, d_model = xall.shape
     n_exp, _, rows, _ = ysall.shape
     per_exp = rows // batch
@@ -108,11 +108,11 @@
 
     def w1_copy(b):
         e, f0 = expert_of(*job_of(b)[:2]), b % blocks * FF_BLOCK
-        return pltpu.make_async_copy(w1_hbm.at[e, :, pl.ds(f0, FF_BLOCK)], w1buf.at[b % ahead], w1_sem.at[b % ahead])
+        return pltpu.make_async_copy(w1_hbm.at[e, :, pl.ds(f0, FF_BLOCK)], w1buf.at[b % ahead], w_sem.at[b % ahead])
 
     def w2_copy(b):
         e, f0 = expert_of(*job_of(b)[:2]), b % blocks * FF_BLOCK
-        return pltpu.make_async_copy(w2_hbm.at[e, pl.ds(f0, FF_BLOCK), :], w2buf.at[b % ahead], w2_sem.at[b % ahead])
+        return pltpu.make_async_copy(w2_hbm.at[e, pl.ds(f0, FF_BLOCK), :], w2buf.at[b % ahead], w_sem.at[b % ahead])
 
     def x_to_pair(k, b):
         src, dst = pl.ds(b * per_exp, per_exp), pl.ds(rows + b * per_exp, per_exp)
@@ -279,9 +279,8 @@
             if kind == "A" and b % blocks == 0:
                 whole = xpair.at[k, pl.ds(rows, rows)]
                 pltpu.make_async_remote_copy(src_ref=whole, dst_ref=whole, send_sem=xp_send.at[0], recv_sem=xp_recv.at[k], device_id={"data": pair}, device_id_type=MESH).wait_recv()
-            w1_copy(b).wait()
-        for b in seconds:
-            w2_copy(b).wait()
+            both = w1buf.at[pl.ds(0, 2)]
+            pltpu.make_async_copy(both, both, w_sem.at[b % ahead]).wait()
         for b in sorted({*firsts, *(b + 1 for b in seconds)}):
             if b in firsts:
                 kind, k, only = job_of(b)
@@ -407,7 +406,7 @@
                 pltpu.VMEM((batch * toks, d_model), F32),
                 pltpu.VMEM((AHEAD, d_model, FF_BLOCK), BF16),
                 pltpu.VMEM((AHEAD, FF_BLOCK, d_model), BF16),
-                dma((batch + 2,)), dma((AHEAD,)), dma((AHEAD,)),
+                dma((batch + 2,)), dma((AHEAD,)),
                 dma((batch,)), dma((batch, 6)), dma((3,)), dma((len(RINGS), 4)),
                 dma((1,)), dma((SHARED,)), dma((1,)), dma((SHARED,)),
                 pltpu.SMEM((batch,), jnp.int32),

time: 46.1 us -> 46 us (level)
  no operation moved by 1% of the time
where the time goes in v7:
time: 46 us; the launch traced here: 45.9 us
  Pallas kernels  44.6 us (97%)
  local copies, waits for them, and re-layouts  0.71 us (2%)
  between operations  0.66 us (1%)
    pallas_call x1, Pallas kernels, local_layer(): pl.pallas_call(functools.partial(kernel, n), out_shape=pltpu.VMEM(tok_blk...  44.6 us

profile of v7, /device:TPU:113, one launch (start us, length us, event | category | flops | bytes accessed | tf_op | source)
XLA Modules:
  0.0 45.9 jit_solution(2450881497056721788)
XLA Ops:
  0.7 44.6 %shard_map.64 = bf16[2,64,1024]{2,1,0:T(8,128)(2,1)S(1)} custom-call(bf16[2,64,1024]{2,1,0:T(8,128)(2,1)} %tok_hbm.1, s32[2]{0:T(128)} %len_hbm.1, bf16[1024,1024]{1,0:T(8,128)(2,1)} %phi_hbm.1, f32[1]{0:T(128)} %bitcast.1.g_ref, bf16[8,1024,4096]{2,1,0:T(8,128)(2,1)} %w1_hbm.1, bf16[8,4096,1024]{2,1,0:T(8,128)(2,1)} %w2_hbm.1), custom_call_target="tpu_custom_call" | custom-call | tf_op jit(solution)/shard_map/pallas_call | solution.py:387
  45.2 0.7 %copy.8 = bf16[2,64,1024]{2,1,0:T(8,128)(2,1)} copy(bf16[2,64,1024]{2,1,0:T(8,128)(2,1)S(1)} %shard_map.64) | data formatting | bytes 524288
